TPU v7x, 32 devices: a whole 2x2x4 slice. The times are simulated.
32 devices in a mesh: freq: 8 (over z, x), kgrp: 4 (over y, core).
Axes of the slice: x: 2, y: 2, z: 4, core: 2. Of those that a mesh axis runs over, the one named last changes fastest.
Arguments:
- hamiltonian: float32 [256, 64, 128], P(('freq', 'kgrp')), may hold values from -1 to 1, as said below
- self_energy: float32 [16, 64, 128], P('freq'), may hold values from -0.8 to 0.3, as said below
- guess_factor: float32 [16, 64, 128], P('freq'), may hold values from -0.05 to 1.25
- weights: int32 [256], replicated, may hold values from 1 to 48
- counts: int32 [16], replicated, may hold values from 1 to 3, as said below
Outputs:
- local_green: float32 [4096, 32], P(('freq', 'kgrp'))
Inputs may be any that keep to these rules, and one draw needn't show every extreme that they name: `hamiltonian`: each k-point's matrix is Hermitian: the left half symmetric, the right half antisymmetric. `self_energy`: the diagonal of the right half lies between -0.8 and -0.4. `counts`: the number of Newton-Schulz steps taken at each frequency.
All inputs are finite; a program needn't handle non-finite values.
Results may differ from a plain program's by a relative error of at most 0.0001.
Values sent between devices are 32-bit elements.
No kernel may reach another device: no remote copies, remote signals or barrier semaphores. Data moves between devices by JAX's collectives and lax.ppermute only.
A program may use at most 64 MiB of HBM per device.

v0:
```python
import math

import jax
import jax.numpy as jnp
from jax import lax
from jax.sharding import PartitionSpec as P

chem_potential = 0.2


def blockify(right_side):
    order = right_side.shape[-1] // 2
    real_part = right_side[..., :order]
    imag_part = right_side[..., order:]
    upper_row = jnp.concatenate([real_part, imag_part], -1)
    lower_row = jnp.concatenate([-imag_part, real_part], -1)
    return jnp.concatenate([upper_row, lower_row], -2)


def complex_product(left_side, right_side):
    return jnp.einsum(
        "...ij,...jl->...il", left_side, blockify(right_side), precision=lax.Precision.HIGHEST
    )


def build_matrix(kpoint_rows, sigma_rows, matsubara):
    orbitals = kpoint_rows.shape[1]
    identity = jnp.eye(orbitals, dtype=jnp.float32)
    real_shift = jnp.broadcast_to(chem_potential * identity, matsubara.shape + identity.shape)
    imag_shift = matsubara[:, None, None] * identity
    diagonal_shift = jnp.concatenate([real_shift, imag_shift], -1)
    return diagonal_shift[:, None] - kpoint_rows[None] - sigma_rows[:, None]


def start_guess(matrix, factor_rows):
    orbitals = matrix.shape[-2]
    diag_real = jnp.diagonal(matrix[..., :orbitals], axis1=-2, axis2=-1)
    diag_imag = jnp.diagonal(matrix[..., orbitals:], axis1=-2, axis2=-1)
    modulus = diag_real * diag_real + diag_imag * diag_imag
    recip_real = (diag_real / modulus)[..., None]
    recip_imag = (-diag_imag / modulus)[..., None]
    factor_real = factor_rows[..., :orbitals]
    factor_imag = factor_rows[..., orbitals:]
    guess_real = recip_real * factor_real - recip_imag * factor_imag
    guess_imag = recip_real * factor_imag + recip_imag * factor_real
    return jnp.concatenate([guess_real, guess_imag], -1)


def invert_blocks(kpoint_rows, sigma_rows, factor_rows, freq_ids, freq_total, step_counts):
    orbitals = kpoint_rows.shape[1]
    matsubara = (2 * freq_ids + 1).astype(jnp.float32) * (math.pi / (2 * freq_total))
    matrix = build_matrix(kpoint_rows, sigma_rows, matsubara)
    initial = start_guess(matrix, factor_rows[:, None])
    identity = jnp.eye(orbitals, dtype=jnp.float32)
    doubled = jnp.concatenate([2.0 * identity, jnp.zeros_like(identity)], -1)
    longest = jnp.max(step_counts)

    def newton_step(sweep, current):
        updated = complex_product(current, doubled - complex_product(matrix, current))
        active = (sweep < step_counts)[:, None, None, None]
        return jnp.where(active, updated, current)

    return lax.fori_loop(0, longest, newton_step, initial)


def per_device(hamiltonian, self_energy, guess_factor, weights, counts):
    orbitals = hamiltonian.shape[1]
    per_freq = self_energy.shape[0]
    k_local = hamiltonian.shape[0]
    freq_devs = lax.axis_size("freq")
    group_devs = lax.axis_size("kgrp")
    freq_total = per_freq * freq_devs
    pair_block = orbitals * orbitals // (freq_devs * group_devs)
    freq_pos = lax.axis_index("freq")
    group_pos = lax.axis_index("kgrp")
    weight_total = jnp.sum(weights.astype(jnp.float32))
    first_freq = freq_pos * per_freq
    freq_ids = first_freq + jnp.arange(per_freq, dtype=jnp.int32)
    local_counts = lax.dynamic_slice_in_dim(counts, first_freq, per_freq)
    empty = jnp.zeros((per_freq, orbitals, 2 * orbitals), jnp.float32)
    h_piece = lax.all_gather(hamiltonian, "freq", axis=0, tiled=True)
    row_ids = jnp.arange(h_piece.shape[0], dtype=jnp.int32)
    kpoint_ids = (
        row_ids // k_local * (group_devs * k_local) + group_pos * k_local + row_ids % k_local
    )
    factors = jnp.take(weights, kpoint_ids).astype(jnp.float32)
    inverses = invert_blocks(h_piece, self_energy, guess_factor, freq_ids, freq_total, local_counts)
    partial_sum = empty + jnp.einsum(
        "k,fkij->fij", factors, inverses, precision=lax.Precision.HIGHEST
    )
    partial_term = partial_sum.reshape(per_freq, orbitals, 2, orbitals).transpose(0, 2, 1, 3)
    partial_term = partial_term.reshape(per_freq, 2, freq_devs, group_devs, pair_block)
    quarter = lax.psum_scatter(partial_term, "kgrp", scatter_dimension=3, tiled=True)
    own_block = lax.all_to_all(quarter, "freq", split_axis=2, concat_axis=0, tiled=True)
    result = own_block.reshape(freq_total, 2, pair_block).transpose(2, 1, 0)
    result = result.reshape(pair_block, 2 * freq_total)
    return result / weight_total


def solution(mesh):
    return jax.shard_map(
        per_device,
        mesh=mesh,
        in_specs=(
            P(("freq", "kgrp"), None, None),
            P("freq", None, None),
            P("freq", None, None),
            P(),
            P(),
        ),
        out_specs=P(("freq", "kgrp"), None),
        check_vma=False,
    )
```

profile of v0, /device:TPU:0, one launch (start us, length us, event | category | flops | bytes accessed | tf_op | source)
XLA Modules:
  0.0 254.6 jit_solution(18190789245727477502)
XLA Ops:
  7.6 2.6 %copy.25 = f32[2,64,128]{0,2,1:T(8,128)} copy(f32[2,64,128]{2,1,0:T(8,128)S(1)} %pad_maximum_fusion.1) | data formatting | bytes 131072 | tf_op jit(solution)/shard_map/concatenate | solution.py:31
  10.2 2.6 %copy.27 = f32[2,64,128]{0,2,1:T(8,128)} copy(f32[2,64,128]{2,1,0:T(8,128)S(1)} %copy-done.2) | data formatting | bytes 131072 | tf_op args[1]
  14.5 46.8 %all-gather.2.cloned.1.call-done = f32[64,64,128]{2,1,0:T(8,128)} async-done(((f32[8,64,128]{2,1,0:T(8,128)}), f32[64,64,128]{2,1,0:T(8,128)}) %all-gather.2.cloned.1.call-update) | async-done | bytes 2097168 | tf_op jit(solution)/shard_map/all_gather | solution.py:81
  61.3 3.8 %copy.26 = f32[64,64,128]{0,2,1:T(8,128)} copy(f32[64,64,128]{2,1,0:T(8,128)} %all-gather.2.cloned.1.call-done) | data formatting | bytes 4194304 | tf_op jit(solution)/shard_map/all_gather | solution.py:81
  65.1 22.3 %subtract_subtract_fusion = f32[2,64,64,128]{1,0,3,2:T(2,128)} fusion(f32[2,64,128]{0,2,1:T(8,128)} %copy.27, f32[64,64,128]{0,2,1:T(8,128)} %copy.26, f32[2,64,128]{0,2,1:T(8,128)} %copy.25), kind=kLoop, calls=%fused_computation.30 | loop fusion | flops 2097152 | bytes 6422528 | tf_op jit(solution)/shard_map/sub | solution.py:32
  87.4 7.8 %fusion.64 = (f32[2,64,64,64]{1,0,3,2:T(2,128)}, f32[2,64,64,64]{1,0,3,2:T(2,128)}) fusion(f32[2,64,64,128]{1,0,3,2:T(2,128)} %subtract_subtract_fusion), kind=kLoop, calls=%fused_computation.96 | loop fusion | bytes 8388608 | tf_op jit(solution)/shard_map/slice | solution.py:37
  95.3 2.9 %gather_fusion.1 = f32[64,2,64]{2,1,0:T(2,128)S(1)} fusion(f32[2,64,64,64]{1,0,3,2:T(2,128)} %get-tuple-element.83, s32[64]{0:T(128)S(1)} %or_bitcast_fusion), kind=kCustom, calls=%fused_computation.1 | custom fusion | bytes 66048 | tf_op jit(solution)/shard_map/jit(diagonal)/gather | solution.py:37
  98.3 3.0 %gather_fusion.2 = f32[64,2,64]{2,1,0:T(2,128)S(1)} fusion(f32[2,64,64,64]{1,0,3,2:T(2,128)} %get-tuple-element.84, s32[64]{0:T(128)S(1)} %or_bitcast_fusion), kind=kCustom, calls=%fused_computation.2 | custom fusion | bytes 66048 | tf_op jit(solution)/shard_map/jit(diagonal)/gather | solution.py:38
  103.7 3.1 %pad_maximum_fusion = f32[2,64,64,128]{3,2,1,0:T(8,128)} fusion(f32[2,64,64,64]{3,2,1,0:T(8,128)S(1)} %get-tuple-element.86, f32[2,64,64,64]{3,2,1,0:T(8,128)S(1)} %get-tuple-element.85), kind=kLoop, calls=%fused_computation.31 | loop fusion | flops 1048576 | bytes 8388608 | tf_op jit(solution)/shard_map/concatenate | solution.py:46
  106.8 87.1 %while.11 = (s32[]{:T(128)}, f32[2,64,64,128]{3,2,1,0:T(8,128)}, s32[]{:T(128)}, s32[2]{0:T(128)S(1)}, f32[64,128]{1,0:T(8,128)S(1)}, /*index=5*/f32[64,64,128]{...) while((s32[]{:T(128)}, f32[2,64,64,128]{3,2,1,0:T(8,128)}, ...), condition=%wide.region_2.3_spmd.clone, body=%wide.region_1.2_spmd.clone.sunk | while | flops 3234856960 | bytes 56787048 | solution.py:63
  111.3 8.9 %bitcast_subtract_fusion.2 = f32[2,64,64,128]{3,2,1,0:T(8,128)S(1)} fusion(f32[64,128]{1,0:T(8,128)S(1)} %get-tuple-element.171, f32[2,64,128]{2,1,0:T(8,128)S(1)} %get-tuple-element.174, f32[64,64,128]{2,1,0:T(8,128)S(1)} %get-tuple-element.172, f32[2,64,128]{2,1,0:T(8,128)S(1)} %get-tuple-element.173, ...), kind=kOutput, calls=%fused_computation.18.clone.1 | convolution fusion | flops 1617952768 | bytes 14843904 | tf_op jit(solution)/shard_map/while/body/...ij,...jl->...il/dot_general | solution.py:21
  120.2 3.5 %slice_negate_fusion.5 = (f32[2,64,64,64]{3,2,1,0:T(8,128)S(1)}, f32[2,64,64,64]{3,2,1,0:T(8,128)}) fusion(f32[2,64,64,128]{3,2,1,0:T(8,128)S(1)} %bitcast_subtract_fusion.2), kind=kLoop, calls=%fused_computation.16.clone.1 | loop fusion | flops 524288 | bytes 8388608 | tf_op jit(solution)/shard_map/while/body/neg | solution.py:16
  123.7 11.9 %bitcast_select_fusion.2 = f32[2,64,64,128]{3,2,1,0:T(8,128)} fusion(f32[2,64,64,128]{3,2,1,0:T(8,128)S(1)} %copy.51, f32[2,64,64,64]{3,2,1,0:T(8,128)} %get-tuple-element.147, f32[2,64,64,64]{3,2,1,0:T(8,128)S(1)} %get-tuple-element.148, f32[2,64,64,128]{3,2,1,0:T(8,128)S(1)} %bitcast_subtract_fusion.2, pred[2]{0:T(512)(128)(4,1)S(1)} %broadcast_compare_fusion.2), kind=kOutput, calls=%fused_computation.17.clone.1 | convolution fusion | flops 1615855616 | bytes 16777218 | tf_op jit(solution)/shard_map/while/body/...ij,...jl->...il/dot_general | solution.py:21
  139.9 8.9 %bitcast_subtract_fusion.2 = f32[2,64,64,128]{3,2,1,0:T(8,128)S(1)} fusion(f32[64,128]{1,0:T(8,128)S(1)} %get-tuple-element.171, f32[2,64,128]{2,1,0:T(8,128)S(1)} %get-tuple-element.174, f32[64,64,128]{2,1,0:T(8,128)S(1)} %get-tuple-element.172, f32[2,64,128]{2,1,0:T(8,128)S(1)} %get-tuple-element.173, ...), kind=kOutput, calls=%fused_computation.18.clone.1 | convolution fusion | flops 1617952768 | bytes 14843904 | tf_op jit(solution)/shard_map/while/body/...ij,...jl->...il/dot_general | solution.py:21
  148.9 3.5 %slice_negate_fusion.5 = (f32[2,64,64,64]{3,2,1,0:T(8,128)S(1)}, f32[2,64,64,64]{3,2,1,0:T(8,128)}) fusion(f32[2,64,64,128]{3,2,1,0:T(8,128)S(1)} %bitcast_subtract_fusion.2), kind=kLoop, calls=%fused_computation.16.clone.1 | loop fusion | flops 524288 | bytes 8388608 | tf_op jit(solution)/shard_map/while/body/neg | solution.py:16
  152.4 11.9 %bitcast_select_fusion.2 = f32[2,64,64,128]{3,2,1,0:T(8,128)} fusion(f32[2,64,64,128]{3,2,1,0:T(8,128)S(1)} %copy.51, f32[2,64,64,64]{3,2,1,0:T(8,128)} %get-tuple-element.147, f32[2,64,64,64]{3,2,1,0:T(8,128)S(1)} %get-tuple-element.148, f32[2,64,64,128]{3,2,1,0:T(8,128)S(1)} %bitcast_subtract_fusion.2, pred[2]{0:T(512)(128)(4,1)S(1)} %broadcast_compare_fusion.2), kind=kOutput, calls=%fused_computation.17.clone.1 | convolution fusion | flops 1615855616 | bytes 16777218 | tf_op jit(solution)/shard_map/while/body/...ij,...jl->...il/dot_general | solution.py:21
  168.6 8.9 %bitcast_subtract_fusion.2 = f32[2,64,64,128]{3,2,1,0:T(8,128)S(1)} fusion(f32[64,128]{1,0:T(8,128)S(1)} %get-tuple-element.171, f32[2,64,128]{2,1,0:T(8,128)S(1)} %get-tuple-element.174, f32[64,64,128]{2,1,0:T(8,128)S(1)} %get-tuple-element.172, f32[2,64,128]{2,1,0:T(8,128)S(1)} %get-tuple-element.173, ...), kind=kOutput, calls=%fused_computation.18.clone.1 | convolution fusion | flops 1617952768 | bytes 14843904 | tf_op jit(solution)/shard_map/while/body/...ij,...jl->...il/dot_general | solution.py:21
  177.6 3.5 %slice_negate_fusion.5 = (f32[2,64,64,64]{3,2,1,0:T(8,128)S(1)}, f32[2,64,64,64]{3,2,1,0:T(8,128)}) fusion(f32[2,64,64,128]{3,2,1,0:T(8,128)S(1)} %bitcast_subtract_fusion.2), kind=kLoop, calls=%fused_computation.16.clone.1 | loop fusion | flops 524288 | bytes 8388608 | tf_op jit(solution)/shard_map/while/body/neg | solution.py:16
  181.1 11.9 %bitcast_select_fusion.2 = f32[2,64,64,128]{3,2,1,0:T(8,128)} fusion(f32[2,64,64,128]{3,2,1,0:T(8,128)S(1)} %copy.51, f32[2,64,64,64]{3,2,1,0:T(8,128)} %get-tuple-element.147, f32[2,64,64,64]{3,2,1,0:T(8,128)S(1)} %get-tuple-element.148, f32[2,64,64,128]{3,2,1,0:T(8,128)S(1)} %bitcast_subtract_fusion.2, pred[2]{0:T(512)(128)(4,1)S(1)} %broadcast_compare_fusion.2), kind=kOutput, calls=%fused_computation.17.clone.1 | convolution fusion | flops 1615855616 | bytes 16777218 | tf_op jit(solution)/shard_map/while/body/...ij,...jl->...il/dot_general | solution.py:21
  193.9 9.2 %dot_general.18 = f32[2,64,2,64,64]{3,2,1,4,0:T(2,128)} reshape(f32[2,64,128,64]{2,1,3,0:T(8,128)} %bitcast.62) | data formatting | bytes 8388608 | tf_op jit(solution)/shard_map/k,fkij->fij/dot_general | solution.py:88
  203.1 12.3 %fusion.27 = f32[1,2,64,2,64]{4,0,3,2,1:T(1,128)S(1)} fusion(f32[2,64,2,64,64]{3,2,1,4,0:T(2,128)} %dot_general.18, s32[64]{0:T(128)S(1)} %gather_fusion, s32[]{:T(128)S(6)} %mul.134), kind=kOutput, calls=%fused_computation.28 | convolution fusion | flops 12584384 | bytes 4260100 | tf_op jit(solution)/shard_map/k,fkij->fij/dot_general | solution.py:88
  216.1 16.9 %reduce-scatter.2.cloned.1.call-done = f32[2,2,8,1,128]{4,2,1,0,3:T(8,128)} async-done(((f32[2,2,8,4,128]{4,2,1,0,3:T(8,128)}), f32[2,2,8,1,128]{4,2,1,0,3:T(8,128)}) %reduce-scatter.2.cloned.1.call-update) | async-done | bytes 16400 | tf_op jit(solution)/shard_map/reduce_scatter | solution.py:93
  234.4 5.5 %all-to-all-start = ((f32[2,2,8,1,128]{4,3,1,0,2:T(1,128)}), f32[2,2,8,1,128]{4,3,1,0,2:T(1,128)S(1)}, u32[]{:S(2)}, u32[]{:S(2)}) async-start(f32[2,2,8,1,128]{4,3,1,0,2:T(1,128)} %copy.33), calls=%async_computation.1 | async-start | bytes 32768 | tf_op jit(solution)/shard_map/all_to_all | solution.py:94
  240.5 6.0 %all-to-all-done = f32[2,2,8,1,128]{4,3,1,0,2:T(1,128)S(1)} async-done(((f32[2,2,8,1,128]{4,3,1,0,2:T(1,128)}), f32[2,2,8,1,128]{4,3,1,0,2:T(1,128)S(1)}, u32[]{:S(2)}, u32[]{:S(2)}) %all-to-all-start) | async-done | bytes 16416 | tf_op jit(solution)/shard_map/all_to_all | solution.py:94
  (48 shorter events, 19.9 us)
Async XLA Ops:
  6.5 3.6 %copy-start.2 = (f32[2,64,128]{2,1,0:T(8,128)S(1)}, f32[2,64,128]{2,1,0:T(8,128)}, u32[]{:S(2)}) copy-start(f32[2,64,128]{2,1,0:T(8,128)} %param.8) | copy-start | bytes 196612
  6.5 54.8 %all-gather.2.cloned.1.call-start = ((), (), s32[]{:S(2)}) async-start(), calls=%async_computation.2 | async-start | bytes 2359296 | tf_op jit(solution)/shard_map/all_gather | solution.py:81
  7.3 225.8 %reduce-scatter.2.cloned.1.call-start = ((), (), s32[]{:S(2)}) async-start(), calls=%async_computation.3 | async-start | bytes 81920 | tf_op jit(solution)/shard_map/reduce_scatter | solution.py:93
  7.5 5.3 %copy-start = (s32[256]{0:T(256)S(1)}, s32[256]{0:T(256)}, u32[]{:S(2)}) copy-start(s32[256]{0:T(256)} %param.10) | copy-start | bytes 3076
  7.5 6.1 %copy-start.4 = (s32[16]{0:T(128)S(1)}, s32[16]{0:T(128)}, u32[]{:S(2)}) copy-start(s32[16]{0:T(128)} %param.11) | copy-start | bytes 196
  7.6 6.8 %copy-start.3 = (f32[2,64,128]{2,1,0:T(8,128)S(1)}, f32[2,64,128]{2,1,0:T(8,128)}, u32[]{:S(2)}) copy-start(f32[2,64,128]{2,1,0:T(8,128)} %param.9) | copy-start | bytes 196612
  103.7 3.1 %copy-start.1 = (f32[64,64,128]{2,1,0:T(8,128)S(1)}, f32[64,64,128]{2,1,0:T(8,128)}, u32[]{:S(2)}) copy-start(f32[64,64,128]{2,1,0:T(8,128)} %all-gather.2.cloned.1.call-done) | copy-start | bytes 6291460
  234.4 12.1 %all-to-all-start = ((f32[2,2,8,1,128]{4,3,1,0,2:T(1,128)}), f32[2,2,8,1,128]{4,3,1,0,2:T(1,128)S(1)}, u32[]{:S(2)}, u32[]{:S(2)}) async-start(f32[2,2,8,1,128]{4,3,1,0,2:T(1,128)} %copy.33), calls=%async_computation.1 | async-start | bytes 32768 | tf_op jit(solution)/shard_map/all_to_all | solution.py:94
Sparse Core Ops, SparseCore 0:
  9.5 51.7 all-gather.1
  216.2 16.7 reduce-scatter.1
where the time goes:
time: 255 us
  matrix products  74.9 us (29%)
  waiting for transfers between devices  70.5 us (28%)
  other arithmetic  44.8 us (18%)
  local copies, waits for them, and re-layouts  42.3 us (17%)
  between operations  13.6 us (5%)
  starting transfers between devices  5.57 us (2%)
  loops' own time  3.03 us (1%)
    dot_general x6, matrix products, complex_product(): jnp.einsum('...ij,...jl->...il', left_side, blockify(right_side), precisi...  62.6 us
    all_gather x1, waiting for transfers between devices, per_device(): h_piece = lax.all_gather(hamiltonian, 'freq', axis=0, tiled=True)  46.8 us
    sub x1, other arithmetic, build_matrix(): return diagonal_shift[:, None] - kpoint_rows[None] - sigma_rows[:, None]  22.3 us
    reduce_scatter x1, waiting for transfers between devices, per_device(): lax.psum_scatter(partial_term, 'kgrp', scatter_dimension=3, tiled=True)  16.9 us
    neg x6, other arithmetic, blockify(): lower_row = jnp.concatenate([-imag_part, real_part], -1)  14.8 us
    dot_general x1, matrix products, per_device(): jnp.einsum('k,fkij->fij', factors, inverses, precision=lax.Precision.HIGH...  12.3 us
    dot_general x2, local copies, waits for them, and re-layouts, per_device(): jnp.einsum('k,fkij->fij', factors, inverses, precision=lax.Precision.HIGH...  9.2 us
    slice x1, local copies, waits for them, and re-layouts, start_guess(): diag_real = jnp.diagonal(matrix[..., :orbitals], axis1=-2, axis2=-1)  7.83 us
  transfers between devices with their start and end apart: 3, of which 3 were waited for; matrix products, arithmetic and copies ran while one was open for 3% of the time, Pallas kernels for 0%

commit v1 on v0

v1 whole, which is shorter than its diff:
```python
import functools
import math

import jax
import jax.numpy as jnp
from jax import lax
from jax.experimental import pallas as pl
from jax.experimental.pallas import tpu as pltpu
from jax.sharding import PartitionSpec as P

chem_potential = 0.2


def is_power_of_two(number):
    return number & (number - 1) == 0


def split_bf16(values):
    high = values.astype(jnp.bfloat16)
    low = (values - high.astype(jnp.float32)).astype(jnp.bfloat16)
    return high, low


def left_operand(values):
    high, low = split_bf16(values)
    return jnp.concatenate([high, low], -1)


def right_operand(values, swap_sign):
    width = values.shape[-1]
    block = jnp.concatenate([values, pltpu.roll(values, width // 2, 1) * swap_sign], 0)
    high, low = split_bf16(block)
    upper = jnp.concatenate([high, low], -1)
    lower = jnp.concatenate([high, jnp.zeros_like(low)], -1)
    return jnp.concatenate([upper, lower], 0)


def product(left, right):
    width = right.shape[-1] // 2
    both = jnp.dot(left, right, preferred_element_type=jnp.float32)
    return both[:, :width] + both[:, width:]


def green_kernel(
    sizes, weights_ref, counts_ref, *refs
):
    (z_devs, x_devs, c_devs, sub, k_local, group_devs, freq_total, orbitals, pieces) = sizes
    h_refs = refs[:pieces]
    sg_refs = refs[pieces:pieces + z_devs]
    out_ref = refs[pieces + z_devs]
    t_ref, hd_ref, wr_ref, g_ref, c_ref, r_ref, plane_ref = refs[pieces + z_devs + 1:]
    width = 2 * orbitals
    freqs = z_devs * sub
    k_total = pieces * k_local
    batch = math.gcd(k_total, 8)
    freq_pos = lax.axis_index("freq")
    group_pos = lax.axis_index("kgrp")
    z_pos, x_pos = freq_pos // x_devs, freq_pos % x_devs
    c_pos = group_pos % c_devs

    row = lax.broadcasted_iota(jnp.int32, (orbitals, width), 0)
    lane = lax.broadcasted_iota(jnp.int32, (orbitals, width), 1)
    in_left = lane < orbitals
    eye_left = (lane == row).astype(jnp.float32)
    eye_both = eye_left + (lane == row + orbitals).astype(jnp.float32)
    lane_row = lax.broadcasted_iota(jnp.int32, (1, width), 1)
    left_row = lane_row < orbitals
    swap_sign = jnp.where(left_row, -1.0, 1.0)

    def swap(values):
        return pltpu.roll(values, orbitals, 1)

    def block_of(step):
        if is_power_of_two(z_devs):
            return z_pos ^ step
        return (z_pos + z_devs - step) % z_devs

    def freq_of(step, member):
        return (block_of(step) * x_devs + x_pos) * (c_devs * sub) + c_pos * sub + member

    for step in range(z_devs):
        for member in range(sub):
            place = step * sub + member
            guess = sg_refs[step][1, member]
            sigma = sg_refs[step][0, member]
            freq_id = freq_of(step, member)
            matsubara = (2 * freq_id + 1).astype(jnp.float32) * (math.pi / (2 * freq_total))
            left = left_operand(guess)
            g_ref[pl.ds(place * orbitals, orbitals), :] = left
            shift = eye_left * chem_potential + (eye_both - eye_left) * matsubara
            c_ref[place] = product(left, right_operand(shift - sigma, swap_sign))

    for piece in range(pieces):
        x_flip, c_flip = piece // c_devs, piece % c_devs
        first_k = ((freq_pos ^ x_flip) * group_devs + (group_pos ^ c_flip)) * k_local

        def load_point(local, carry, piece=piece, first_k=first_k):
            place = piece * k_local + local
            matrix = h_refs[piece][local]
            t_ref[place] = product(g_ref[...], right_operand(matrix, swap_sign))
            diag = jnp.sum(matrix * eye_left, 0, keepdims=True)
            hd_ref[pl.ds(place, 1), :] = diag + swap(diag)
            weight = weights_ref[first_k + local].astype(jnp.float32)
            wr_ref[pl.ds(place, 1), :] = jnp.full((1, width), weight, jnp.float32)
            return carry

        lax.fori_loop(0, k_local, load_point, 0)

    def sum_frequency(place, count, sg_ref, member, freq_id, plane):
        matsubara = (2 * freq_id + 1).astype(jnp.float32) * (math.pi / (2 * freq_total))
        sigma_diag = jnp.sum(sg_ref[0, member] * eye_both, 0, keepdims=True)
        sigma_swap = swap(sigma_diag)
        real_base = chem_potential - jnp.where(left_row, sigma_diag, sigma_swap)
        imag = matsubara - jnp.where(left_row, sigma_swap, sigma_diag)
        constant = c_ref[place]
        r_ref[...] = jnp.zeros_like(r_ref)

        def accumulate(terms):
            def one_batch(step, carry):
                first = step * batch
                first_row = pl.multiple_of(first, batch)
                real = real_base - hd_ref[pl.ds(first_row, 8), :]
                modulus = real * real + imag * imag
                d_real = real / modulus
                d_swap = jnp.broadcast_to(imag, real.shape) / modulus * (-swap_sign)
                weight = wr_ref[pl.ds(first_row, 8), :]
                real_cols = jnp.transpose(d_real * weight)
                swap_cols = jnp.transpose(d_swap * weight)
                errors = []
                for item in range(batch):
                    mixed = constant - t_ref[first + item, pl.ds(place * orbitals, orbitals), :]
                    scaled = mixed * d_real[item:item + 1] + swap(mixed) * d_swap[item:item + 1]
                    errors.append(eye_left - scaled)
                total = r_ref[...]
                for item, series in enumerate(terms(errors)):
                    total = total + series * real_cols[:orbitals, item:item + 1]
                    turned = swap(series) * swap_sign
                    total = total + turned * swap_cols[orbitals:, item:item + 1]
                r_ref[...] = total
                return carry

            lax.fori_loop(0, k_total // batch, one_batch, 0)

        def one_step(errors):
            return [eye_left + error for error in errors]

        def cubic(errors):
            rights = [right_operand(error, swap_sign) for error in errors]
            squares = [product(left_operand(e), r) for e, r in zip(errors, rights)]
            cubes = [product(left_operand(s), r) for s, r in zip(squares, rights)]
            sums = [eye_left + e + s + c for e, s, c in zip(errors, squares, cubes)]
            return rights, cubes, sums

        def two_steps(errors):
            return cubic(errors)[2]

        def three_steps(errors):
            rights, cubes, sums = cubic(errors)
            fourths = [product(left_operand(c), r) for c, r in zip(cubes, rights)]
            lasts = [
                product(left_operand(s), right_operand(f, swap_sign)) for s, f in zip(sums, fourths)
            ]
            return [s + p for s, p in zip(sums, lasts)]

        @pl.when(count <= 1)
        def _():
            accumulate(one_step)

        @pl.when(count == 2)
        def _():
            accumulate(two_steps)

        @pl.when(count >= 3)
        def _():
            accumulate(three_steps)

        guess = sg_ref[1, member]
        r_ref[...] = product(left_operand(r_ref[...]), right_operand(guess, swap_sign))
        half = orbitals // 2
        even = r_ref[pl.ds(0, half, stride=2), :]
        odd = r_ref[pl.ds(1, half, stride=2), :]
        keep = in_left[:half]
        plane_ref[pl.ds(plane * half, half), :] = jnp.where(keep, even, swap(odd))
        plane_ref[pl.ds((freqs + plane) * half, half), :] = jnp.where(keep, swap(even), odd)

    for step in range(z_devs):
        for member in range(sub):
            freq_id = freq_of(step, member)
            sum_frequency(
                step * sub + member,
                counts_ref[freq_id],
                sg_refs[step],
                member,
                freq_id,
                block_of(step) * sub + member,
            )

    half = orbitals // 2
    for line in range(half):
        out_ref[line] = plane_ref[pl.ds(line, 2 * freqs, stride=half), :]


def final_kernel(sizes, weights_ref, parts_ref, out_ref):
    z_devs, x_devs, y_devs, c_devs, sub = sizes
    total = jnp.sum(weights_ref[...].astype(jnp.float32))
    shared = x_devs * c_devs
    for x_pos in range(x_devs):
        for c_pos in range(c_devs):
            gathered = None
            for z_pos in range(z_devs):
                for y_pos in range(y_devs):
                    source = ((z_pos * x_devs + x_pos) * y_devs + y_pos) * c_devs + c_pos
                    part = parts_ref[source]
                    gathered = part if gathered is None else gathered + part
            gathered = gathered / total
            place = x_pos * c_devs + c_pos
            if sub == 1:
                out_ref[pl.ds(place, 2 * z_devs, stride=shared), :] = gathered
            else:
                for group in range(2 * z_devs):
                    out_ref[pl.ds((group * shared + place) * sub, sub), :] = gathered[
                        group * sub:(group + 1) * sub
                    ]


def per_device(hamiltonian, self_energy, guess_factor, weights, counts):
    k_local, orbitals, width = hamiltonian.shape
    per_freq = self_energy.shape[0]
    freq_devs = lax.axis_size("freq")
    group_devs = lax.axis_size("kgrp")
    devices = freq_devs * group_devs
    freq_total = per_freq * freq_devs
    pair_block = orbitals * orbitals // devices
    x_devs = 2 if freq_devs % 2 == 0 else 1
    c_devs = 2 if group_devs % 2 == 0 and per_freq % 2 == 0 else 1
    z_devs = freq_devs // x_devs
    y_devs = group_devs // c_devs
    sub = per_freq // c_devs
    freqs = z_devs * sub
    c_pos = lax.axis_index("kgrp") % c_devs

    def core_flip(values):
        return lax.ppermute(values, "kgrp", [(i, i ^ 1) for i in range(group_devs)])

    def x_flip(values):
        return lax.ppermute(values, "freq", [(i, i ^ 1) for i in range(freq_devs)])

    def z_move(values, step):
        if is_power_of_two(z_devs):
            pairs = [(i, ((i // x_devs) ^ step) * x_devs + i % x_devs) for i in range(freq_devs)]
        else:
            pairs = [
                (i, (i // x_devs + step) % z_devs * x_devs + i % x_devs) for i in range(freq_devs)
            ]
        return lax.ppermute(values, "freq", pairs)

    own = jnp.stack([self_energy, guess_factor])
    own = lax.dynamic_slice_in_dim(own, c_pos * sub, sub, 1)
    sg_blocks = [own] + [z_move(own, step) for step in range(1, z_devs)]
    h_blocks = [hamiltonian]
    if x_devs == 2:
        h_blocks.append(x_flip(hamiltonian))
    if c_devs == 2:
        h_blocks = [piece for block in h_blocks for piece in (block, core_flip(block))]
    pieces = len(h_blocks)
    k_total = pieces * k_local
    k_rows = -(-k_total // 8) * 8

    vmem = pl.BlockSpec(memory_space=pltpu.VMEM)
    smem = pl.BlockSpec(memory_space=pltpu.SMEM)
    half = orbitals // 2
    partial_sums = pl.pallas_call(
        functools.partial(
            green_kernel,
            (z_devs, x_devs, c_devs, sub, k_local, group_devs, freq_total, orbitals, pieces),
        ),
        out_shape=jax.ShapeDtypeStruct((half, 2 * freqs, width), jnp.float32),
        in_specs=[smem, smem] + [vmem] * (pieces + z_devs),
        out_specs=vmem,
        scratch_shapes=[
            pltpu.VMEM((k_total, freqs * orbitals, width), jnp.float32),
            pltpu.VMEM((k_rows, width), jnp.float32),
            pltpu.VMEM((k_rows, width), jnp.float32),
            pltpu.VMEM((freqs * orbitals, 2 * width), jnp.bfloat16),
            pltpu.VMEM((freqs, orbitals, width), jnp.float32),
            pltpu.VMEM((orbitals, width), jnp.float32),
            pltpu.VMEM((2 * freqs * half, width), jnp.float32),
        ],
        compiler_params=pltpu.CompilerParams(vmem_limit_bytes=48 * 1024 * 1024),
        name="green",
    )(weights, counts, *h_blocks, *sg_blocks)

    share = width // pair_block
    outgoing = partial_sums.reshape(half, 2 * freqs, share, pair_block).transpose(0, 2, 1, 3)
    outgoing = outgoing.reshape(devices, 2 * freqs, pair_block)
    arrived = lax.all_to_all(outgoing, ("freq", "kgrp"), 0, 0, tiled=True)
    result = pl.pallas_call(
        functools.partial(final_kernel, (z_devs, x_devs, y_devs, c_devs, sub)),
        out_shape=jax.ShapeDtypeStruct((2 * freq_total, pair_block), jnp.float32),
        in_specs=[vmem, vmem],
        out_specs=vmem,
        name="collect",
    )(weights.reshape(1, -1), arrived)
    return result.T


def solution(mesh):
    return jax.shard_map(
        per_device,
        mesh=mesh,
        in_specs=(
            P(("freq", "kgrp"), None, None),
            P("freq", None, None),
            P("freq", None, None),
            P(),
            P(),
        ),
        out_specs=P(("freq", "kgrp"), None),
        check_vma=False,
    )
```

time: 255 us -> 57.2 us (0.22)
  matrix products: 74.9 us -> 0 us
  waiting for transfers between devices: 70.5 us -> 12 us
  other arithmetic: 44.8 us -> 0.81 us
  local copies, waits for them, and re-layouts: 42.3 us -> 0.95 us
  Pallas kernels: 0 us -> 22.1 us
  between operations: 13.6 us -> 0.04 us
  blocking collectives: 0 us -> 12.9 us
  loops' own time: 3.03 us -> 0 us
    dot_general x7 -> x0, matrix products: 74.9 us -> none  [the longest x6 62.6 us: complex_product(): jnp.einsum('...ij,...jl->...il', left_side, blockify(right_side), precisi...]
    all_gather x1 -> x0, waiting for transfers between devices: 46.8 us -> none  [per_device(): h_piece = lax.all_gather(hamiltonian, 'freq', axis=0, tiled=True)]
    sub x2 -> x0, other arithmetic: 24.6 us -> none  [the longest x1 22.3 us: build_matrix(): return diagonal_shift[:, None] - kpoint_rows[None] - sigma_rows[:, None]]
    pallas_call x0 -> x2, Pallas kernels: none -> 22.1 us  [the longest x1 20.5 us: per_device(): pl.pallas_call(functools.partial(green_kernel, (z_devs, x_devs, c_devs, s...]
    reduce_scatter x1 -> x0, waiting for transfers between devices: 16.9 us -> none  [per_device(): lax.psum_scatter(partial_term, 'kgrp', scatter_dimension=3, tiled=True)]
    neg x6 -> x0, other arithmetic: 14.8 us -> none  [blockify(): lower_row = jnp.concatenate([-imag_part, real_part], -1)]
    all_to_all x0 -> x1, blocking collectives: none -> 12.9 us  [per_device(): arrived = lax.all_to_all(outgoing, ('freq', 'kgrp'), 0, 0, tiled=True)]
    ppermute x0 -> x6, waiting for transfers between devices: none -> 12 us  [the longest x1 6.51 us: x_flip(): return lax.ppermute(values, 'freq', [(i, i ^ 1) for i in range(freq_devs)])]
  transfers between devices with their start and end apart: 3 -> 6, of which waited for: 3 -> 3; matrix products, arithmetic and copies ran while one was open for 3% -> 1% of each run, Pallas kernels for 0% -> 0%
where the time goes in v1:
time: 57.2 us; the launch traced here: 56.3 us
  Pallas kernels  22.1 us (39%)
  blocking collectives  12.9 us (23%)
  waiting for transfers between devices  12 us (21%)
  starting transfers between devices  7.46 us (13%)
  local copies, waits for them, and re-layouts  0.95 us (2%)
  other arithmetic  0.81 us (1%)
    pallas_call x1, Pallas kernels, per_device(): pl.pallas_call(functools.partial(green_kernel, (z_devs, x_devs, c_devs, s...  20.5 us
    all_to_all x1, blocking collectives, per_device(): arrived = lax.all_to_all(outgoing, ('freq', 'kgrp'), 0, 0, tiled=True)  12.9 us
    ppermute x1, waiting for transfers between devices, x_flip(): return lax.ppermute(values, 'freq', [(i, i ^ 1) for i in range(freq_devs)])  6.51 us
    ppermute x3, waiting for transfers between devices, z_move(): return lax.ppermute(values, 'freq', pairs)  5.49 us
    ppermute x3, starting transfers between devices, z_move(): return lax.ppermute(values, 'freq', pairs)  4.49 us
    ppermute x1, starting transfers between devices, x_flip(): return lax.ppermute(values, 'freq', [(i, i ^ 1) for i in range(freq_devs)])  2.97 us
    pallas_call x1, Pallas kernels, per_device(): pl.pallas_call(functools.partial(final_kernel, (z_devs, x_devs, y_devs, c...  1.65 us
  transfers between devices with their start and end apart: 6, of which 3 were waited for; matrix products, arithmetic and copies ran while one was open for 1% of the time, Pallas kernels for 0%

profile of v1, /device:TPU:0, one launch (start us, length us, event | category | flops | bytes accessed | tf_op | source)
XLA Modules:
  0.0 56.3 jit_solution(1136357655312478513)
XLA Ops:
  0.0 3.0 %collective-permute-start.1 = (f32[8,64,128]{2,1,0:T(8,128)}, f32[8,64,128]{2,1,0:T(8,128)S(1)}, u32[]{:S(2)}, u32[]{:S(2)}) collective-permute-start(f32[8,64,128]{2,1,0:T(8,128)} %refs_0_.1), channel_id=1, source_target_pairs={{0,4},{4,0},{8,12},{12,8},{16,20},{20,16},{24,28},{28,24},{1,5},{5... | collective-permute-start | bytes 786440 | tf_op jit(solution)/shard_map/ppermute | solution.py:246
  3.0 0.0 collective-permute-start
  3.0 6.5 %collective-permute-done.1.refs_2_ = f32[8,64,128]{2,1,0:T(8,128)S(1)} collective-permute-done((f32[8,64,128]{2,1,0:T(8,128)}, f32[8,64,128]{2,1,0:T(8,128)S(1)}, u32[]{:S(2)}, u32[]{:S(2)}) %collective-permute-start.1) | collective-permute-done | bytes 262176 | tf_op jit(solution)/shard_map/ppermute | solution.py:246
  9.5 0.0 collective-permute-start.2
  9.5 0.0 copy-start.1
  9.5 0.0 copy-start.2
  9.5 0.8 %fusion.refs_4_ = f32[2,1,64,128]{3,2,1,0:T(8,128)S(1)} fusion(s32[]{:T(128)S(6)} %select_n.11, f32[1,2,64,128]{3,2,1,0:T(8,128)} %bitcast.5, f32[1,2,64,128]{3,2,1,0:T(8,128)} %bitcast.6), kind=kLoop, calls=%fused_computation.2 | loop fusion | flops 16384 | bytes 196612 | tf_op jit(solution)/shard_map/stack | solution.py:257
  10.3 3.9 %collective-permute-start.5 = (f32[2,1,64,128]{3,2,1,0:T(8,128)S(1)}, f32[2,1,64,128]{3,2,1,0:T(8,128)S(1)}, u32[]{:S(2)}, u32[]{:S(2)}) collective-permute-start(f32[2,1,64,128]{3,2,1,0:T(8,128)S(1)} %fusion.refs_4_), channel_id=1, source_target_pairs={{0,24},{4,28},{8,16},{12,20},{16,8},{20,12},{24,0},{28,4},{1,25},{... | collective-permute-start | bytes 196616 | tf_op jit(solution)/shard_map/ppermute | solution.py:255
  14.2 0.0 collective-permute-start.4
  14.2 0.6 %collective-permute-start.3 = (f32[2,1,64,128]{3,2,1,0:T(8,128)S(1)}, f32[2,1,64,128]{3,2,1,0:T(8,128)S(1)}, u32[]{:S(2)}, u32[]{:S(2)}) collective-permute-start(f32[2,1,64,128]{3,2,1,0:T(8,128)S(1)} %fusion.refs_4_), channel_id=1, source_target_pairs={{0,8},{4,12},{8,0},{12,4},{16,24},{20,28},{24,16},{28,20},{1,9},{5... | collective-permute-start | bytes 196616 | tf_op jit(solution)/shard_map/ppermute | solution.py:255
  14.8 2.3 %collective-permute-done.5.refs_7_ = f32[2,1,64,128]{3,2,1,0:T(8,128)S(1)} collective-permute-done((f32[2,1,64,128]{3,2,1,0:T(8,128)S(1)}, f32[2,1,64,128]{3,2,1,0:T(8,128)S(1)}, u32[]{:S(2)}, u32[]{:S(2)}) %collective-permute-start.5) | collective-permute-done | bytes 65568 | tf_op jit(solution)/shard_map/ppermute | solution.py:255
  17.1 3.2 %collective-permute-done.4.refs_6_ = f32[2,1,64,128]{3,2,1,0:T(8,128)S(1)} collective-permute-done((f32[2,1,64,128]{3,2,1,0:T(8,128)S(1)}, f32[2,1,64,128]{3,2,1,0:T(8,128)S(1)}, u32[]{:S(2)}, u32[]{:S(2)}) %collective-permute-start.4) | collective-permute-done | bytes 65568 | tf_op jit(solution)/shard_map/ppermute | solution.py:255
  20.3 0.0 collective-permute-done.3.refs_5_
  20.3 0.0 collective-permute-done.refs_1_
  20.3 0.0 collective-permute-done.2.refs_3_
  20.3 0.0 copy-done.1
  20.3 0.0 copy-done.2
  20.3 0.0 copy-start
  20.3 0.9 %copy-done = f32[8,64,128]{2,1,0:T(8,128)S(1)} copy-done((f32[8,64,128]{2,1,0:T(8,128)S(1)}, f32[8,64,128]{2,1,0:T(8,128)}, u32[]{:S(2)}) %copy-start) | copy-done | bytes 262168
  21.3 20.5 %green.1 = f32[32,8,128]{2,1,0:T(8,128)S(1)} custom-call(s32[256]{0:T(256)S(1)} %copy-done.1, s32[16]{0:T(128)S(1)} %copy-done.2, f32[8,64,128]{2,1,0:T(8,128)S(1)} %copy-done, f32[8,64,128]{2,1,0:T(8,128)S(1)} %collective-permute-done.refs_1_, f32[8,64,128]{2,1,0:T(8,128)S(1)} %collective-permute-done.1.refs_2_, ...), custom_call_target="tpu_custom_call" | custom-call | tf_op jit(solution)/shard_map/green/pallas_call | solution.py:272
  41.8 12.9 %all_to_all.5.parts_ref = f32[32,8,128]{2,1,0:T(8,128)} all-to-all(f32[32,8,128]{2,1,0:T(8,128)S(1)} %green.1), channel_id=1, replica_groups=mesh['freq'=8,'kgrp'=4] {'freq','kgrp'}, dimensions={0} | all-to-all | bytes 262144 | tf_op jit(solution)/shard_map/all_to_all | solution.py:296
  54.7 1.7 %collect.1 = f32[32,128]{1,0:T(8,128)} custom-call(s32[1,256]{1,0:T(1,128)} %bitcast.4, f32[32,8,128]{2,1,0:T(8,128)} %all_to_all.5.parts_ref), custom_call_target="tpu_custom_call" | custom-call | tf_op jit(solution)/shard_map/collect/pallas_call | solution.py:297
Async XLA Ops:
  0.0 9.5 %collective-permute-start.1 = (f32[8,64,128]{2,1,0:T(8,128)}, f32[8,64,128]{2,1,0:T(8,128)S(1)}, u32[]{:S(2)}, u32[]{:S(2)}) collective-permute-start(f32[8,64,128]{2,1,0:T(8,128)} %refs_0_.1), channel_id=1, source_target_pairs={{0,4},{4,0},{8,12},{12,8},{16,20},{20,16},{24,28},{28,24},{1,5},{5... | collective-permute-start | bytes 786440 | tf_op jit(solution)/shard_map/ppermute | solution.py:246
  3.0 17.3 %collective-permute-start = (f32[8,64,128]{2,1,0:T(8,128)}, f32[8,64,128]{2,1,0:T(8,128)S(1)}, u32[]{:S(2)}, u32[]{:S(2)}) collective-permute-start(f32[8,64,128]{2,1,0:T(8,128)} %refs_0_.1), channel_id=1, source_target_pairs={{0,1},{1,0},{2,3},{3,2},{4,5},{5,4},{6,7},{7,6},{8,9},{9,8},{10,11... | collective-permute-start | bytes 786440 | tf_op jit(solution)/shard_map/ppermute | solution.py:243
  9.5 10.8 %collective-permute-start.2 = (f32[8,64,128]{2,1,0:T(8,128)S(1)}, f32[8,64,128]{2,1,0:T(8,128)S(1)}, u32[]{:S(2)}, u32[]{:S(2)}) collective-permute-start(f32[8,64,128]{2,1,0:T(8,128)S(1)} %collective-permute-done.1.refs_2_), channel_id=1, source_target_pairs={{0,1},{1,0},{2,3},{3,2},{4,5},{5,4},{6,7},{7,6},{8,9},{9,8},{10,11... | collective-permute-start | bytes 786440 | tf_op jit(solution)/shard_map/ppermute | solution.py:243
  9.5 10.8 %copy-start.1 = (s32[256]{0:T(256)S(1)}, s32[256]{0:T(256)}, u32[]{:S(2)}) copy-start(s32[256]{0:T(256)} %weights_ref.1) | copy-start | bytes 3076
  9.5 10.8 %copy-start.2 = (s32[16]{0:T(128)S(1)}, s32[16]{0:T(128)}, u32[]{:S(2)}) copy-start(s32[16]{0:T(128)} %counts_ref.1) | copy-start | bytes 196
  10.3 6.8 %collective-permute-start.5 = (f32[2,1,64,128]{3,2,1,0:T(8,128)S(1)}, f32[2,1,64,128]{3,2,1,0:T(8,128)S(1)}, u32[]{:S(2)}, u32[]{:S(2)}) collective-permute-start(f32[2,1,64,128]{3,2,1,0:T(8,128)S(1)} %fusion.refs_4_), channel_id=1, source_target_pairs={{0,24},{4,28},{8,16},{12,20},{16,8},{20,12},{24,0},{28,4},{1,25},{... | collective-permute-start | bytes 196616 | tf_op jit(solution)/shard_map/ppermute | solution.py:255
  14.2 6.1 %collective-permute-start.4 = (f32[2,1,64,128]{3,2,1,0:T(8,128)S(1)}, f32[2,1,64,128]{3,2,1,0:T(8,128)S(1)}, u32[]{:S(2)}, u32[]{:S(2)}) collective-permute-start(f32[2,1,64,128]{3,2,1,0:T(8,128)S(1)} %fusion.refs_4_), channel_id=1, source_target_pairs={{0,16},{4,20},{8,24},{12,28},{16,0},{20,4},{24,8},{28,12},{1,17},{... | collective-permute-start | bytes 196616 | tf_op jit(solution)/shard_map/ppermute | solution.py:255
  14.2 6.1 %collective-permute-start.3 = (f32[2,1,64,128]{3,2,1,0:T(8,128)S(1)}, f32[2,1,64,128]{3,2,1,0:T(8,128)S(1)}, u32[]{:S(2)}, u32[]{:S(2)}) collective-permute-start(f32[2,1,64,128]{3,2,1,0:T(8,128)S(1)} %fusion.refs_4_), channel_id=1, source_target_pairs={{0,8},{4,12},{8,0},{12,4},{16,24},{20,28},{24,16},{28,20},{1,9},{5... | collective-permute-start | bytes 196616 | tf_op jit(solution)/shard_map/ppermute | solution.py:255
  20.3 1.0 %copy-start = (f32[8,64,128]{2,1,0:T(8,128)S(1)}, f32[8,64,128]{2,1,0:T(8,128)}, u32[]{:S(2)}) copy-start(f32[8,64,128]{2,1,0:T(8,128)} %refs_0_.1) | copy-start | bytes 786436

commit v2 on v1

v2 whole, which is shorter than its diff:
```python
import functools
import math

import jax
import jax.numpy as jnp
from jax import lax
from jax.experimental import pallas as pl
from jax.experimental.pallas import tpu as pltpu
from jax.sharding import PartitionSpec as P

chem_potential = 0.2
BATCH = 8
LOAD_BATCH = 8


def is_power_of_two(number):
    return number & (number - 1) == 0


def split_bf16(values):
    high = values.astype(jnp.bfloat16)
    low = (values - high.astype(jnp.float32)).astype(jnp.bfloat16)
    return high, low


def left_operand(values):
    high, low = split_bf16(values)
    return jnp.concatenate([high, low], -1)


def right_operand(values, swap_sign):
    width = values.shape[-1]
    block = jnp.concatenate([values, pltpu.roll(values, width // 2, 1) * swap_sign], 0)
    high, low = split_bf16(block)
    upper = jnp.concatenate([high, low], -1)
    lower = jnp.concatenate([high, jnp.zeros_like(low)], -1)
    return jnp.concatenate([upper, lower], 0)


def product(left, right):
    width = right.shape[-1] // 2
    both = jnp.dot(left, right, preferred_element_type=jnp.float32)
    return both[:, :width] + both[:, width:]


def green_kernel(sizes, first, weights_ref, counts_ref, *refs):
    (z_devs, x_devs, c_devs, sub, k_local, group_devs, freq_total, orbitals, flips) = sizes
    pieces = len(flips)
    width = 2 * orbitals
    half = orbitals // 2
    freqs = z_devs * sub
    k_total = pieces * k_local
    freq_pos = lax.axis_index("freq")
    group_pos = lax.axis_index("kgrp")
    z_pos, x_pos = freq_pos // x_devs, freq_pos % x_devs
    c_pos = group_pos % c_devs

    h_refs, refs = refs[:pieces], refs[pieces:]
    if first:
        sg_refs, refs = refs[:z_devs], refs[z_devs:]
        (sum_ref, left_ref, right_ref, shift_ref, rows_ref), refs = refs[:5], refs[5:]
        t_ref, hd_ref, wr_ref = refs
    else:
        (old_ref, left_ref, right_ref, shift_ref, rows_ref), refs = refs[:5], refs[5:]
        out_ref, t_ref, hd_ref, wr_ref, r_ref, plane_ref = refs

    row = lax.broadcasted_iota(jnp.int32, (orbitals, width), 0)
    lane = lax.broadcasted_iota(jnp.int32, (orbitals, width), 1)
    eye_left = (lane == row).astype(jnp.float32)
    eye_both = eye_left + (lane == row + orbitals).astype(jnp.float32)
    lane_row = lax.broadcasted_iota(jnp.int32, (1, width), 1)
    left_row = lane_row < orbitals
    swap_sign = jnp.where(left_row, -1.0, 1.0)

    def swap(values):
        return pltpu.roll(values, orbitals, 1)

    def block_of(step):
        if is_power_of_two(z_devs):
            return z_pos ^ step
        return (z_pos + z_devs - step) % z_devs

    def freq_of(place):
        step, member = place // sub, place % sub
        return (block_of(step) * x_devs + x_pos) * (c_devs * sub) + c_pos * sub + member

    if first:
        for place in range(freqs):
            step, member = place // sub, place % sub
            sigma = sg_refs[step][0, member]
            guess = sg_refs[step][1, member]
            matsubara = (2 * freq_of(place) + 1).astype(jnp.float32) * (math.pi / (2 * freq_total))
            left = left_operand(guess)
            left_ref[pl.ds(place * orbitals, orbitals), :] = left
            right_ref[place] = right_operand(guess, swap_sign)
            energy = eye_left * chem_potential + (eye_both - eye_left) * matsubara
            shift_ref[place] = product(left, right_operand(energy - sigma, swap_sign))
            sigma_diag = jnp.sum(sigma * eye_both, 0, keepdims=True)
            sigma_swap = swap(sigma_diag)
            rows_ref[place, pl.ds(0, 1), :] = chem_potential - jnp.where(
                left_row, sigma_diag, sigma_swap
            )
            rows_ref[place, pl.ds(1, 1), :] = matsubara - jnp.where(left_row, sigma_swap, sigma_diag)

    def load_points(piece, locals_):
        x_flip, c_flip = flips[piece]
        first_k = ((freq_pos ^ x_flip) * group_devs + (group_pos ^ c_flip)) * k_local
        rights = []
        for local in locals_:
            place = piece * k_local + local
            matrix = h_refs[piece][local]
            rights.append(right_operand(matrix, swap_sign))
            diag = jnp.sum(matrix * eye_left, 0, keepdims=True)
            hd_ref[pl.ds(place, 1), :] = diag + swap(diag)
            weight = weights_ref[first_k + local].astype(jnp.float32)
            wr_ref[pl.ds(place, 1), :] = jnp.full((1, width), weight, jnp.float32)
        for local, right in zip(locals_, rights):
            t_ref[piece * k_local + local] = product(left_ref[...], right)

    for piece in range(pieces):
        for start in range(0, k_local, LOAD_BATCH):
            load_points(piece, range(start, min(start + LOAD_BATCH, k_local)))

    def one_frequency(place, carry):
        real_base = rows_ref[place, pl.ds(0, 1), :]
        imag = rows_ref[place, pl.ds(1, 1), :]
        constant = shift_ref[place]
        count = counts_ref[freq_of(place)]
        real = real_base - hd_ref[...]
        modulus = real * real + imag * imag
        d_real = real / modulus
        d_swap = jnp.broadcast_to(imag, real.shape) / modulus * (-swap_sign)
        real_cols = jnp.transpose(d_real * wr_ref[...])
        swap_cols = jnp.transpose(d_swap * wr_ref[...])
        offset = pl.multiple_of(place * orbitals, orbitals)

        def accumulate(terms):
            total = jnp.zeros((orbitals, width), jnp.float32) if first else old_ref[place]
            for begin in range(0, k_total, BATCH):
                items = range(begin, min(begin + BATCH, k_total))
                errors = []
                for item in items:
                    mixed = constant - t_ref[item, pl.ds(offset, orbitals), :]
                    scaled = mixed * d_real[item:item + 1] + swap(mixed) * d_swap[item:item + 1]
                    errors.append(eye_left - scaled)
                for item, series in zip(items, terms(errors)):
                    total = total + series * real_cols[:orbitals, item:item + 1]
                    turned = swap(series) * swap_sign
                    total = total + turned * swap_cols[orbitals:, item:item + 1]
            if first:
                sum_ref[place] = total
            else:
                r_ref[...] = product(left_operand(total), right_ref[place])

        def one_step(errors):
            return [eye_left + error for error in errors]

        def two_steps(errors):
            rights = [right_operand(e, swap_sign) for e in errors]
            squares = [product(left_operand(e), r) for e, r in zip(errors, rights)]
            cubes = [product(left_operand(s), r) for s, r in zip(squares, rights)]
            return [eye_left + e + s + c for e, s, c in zip(errors, squares, cubes)]

        def three_steps(errors):
            rights = [right_operand(e, swap_sign) for e in errors]
            squares = [product(left_operand(e), r) for e, r in zip(errors, rights)]
            starts = [eye_left + e for e in errors]
            pairs = [jnp.concatenate([a, s], 0) for a, s in zip(starts, squares)]
            both = [
                product(left_operand(p), right_operand(s, swap_sign)) for p, s in zip(pairs, squares)
            ]
            sums = [a + b[:orbitals] for a, b in zip(starts, both)]
            lasts = [
                product(left_operand(s), right_operand(b[orbitals:], swap_sign))
                for s, b in zip(sums, both)
            ]
            return [s + p for s, p in zip(sums, lasts)]

        @pl.when(count <= 1)
        def _():
            accumulate(one_step)

        @pl.when(count == 2)
        def _():
            accumulate(two_steps)

        @pl.when(count >= 3)
        def _():
            accumulate(three_steps)

        if not first:
            even = r_ref[pl.ds(0, half, stride=2), :]
            odd = r_ref[pl.ds(1, half, stride=2), :]
            plane = block_of(place // sub) * sub + place % sub
            real_rows = pl.multiple_of(plane * half, half)
            imag_rows = pl.multiple_of((freqs + plane) * half, half)
            plane_ref[pl.ds(real_rows, half), :] = jnp.where(left_row, even, swap(odd))
            plane_ref[pl.ds(imag_rows, half), :] = jnp.where(left_row, swap(even), odd)
        return carry

    lax.fori_loop(0, freqs, one_frequency, 0)

    if not first:
        for line in range(half):
            out_ref[line] = plane_ref[pl.ds(line, 2 * freqs, stride=half), :]


def final_kernel(sizes, weights_ref, parts_ref, out_ref):
    z_devs, x_devs, y_devs, c_devs, sub = sizes
    total = jnp.sum(weights_ref[...].astype(jnp.float32))
    shared = x_devs * c_devs
    for x_pos in range(x_devs):
        for c_pos in range(c_devs):
            gathered = None
            for z_pos in range(z_devs):
                for y_pos in range(y_devs):
                    source = ((z_pos * x_devs + x_pos) * y_devs + y_pos) * c_devs + c_pos
                    part = parts_ref[source]
                    gathered = part if gathered is None else gathered + part
            gathered = gathered / total
            place = x_pos * c_devs + c_pos
            if sub == 1:
                out_ref[pl.ds(place, 2 * z_devs, stride=shared), :] = gathered
            else:
                for group in range(2 * z_devs):
                    out_ref[pl.ds((group * shared + place) * sub, sub), :] = gathered[
                        group * sub:(group + 1) * sub
                    ]


def per_device(hamiltonian, self_energy, guess_factor, weights, counts):
    k_local, orbitals, width = hamiltonian.shape
    per_freq = self_energy.shape[0]
    freq_devs = lax.axis_size("freq")
    group_devs = lax.axis_size("kgrp")
    devices = freq_devs * group_devs
    freq_total = per_freq * freq_devs
    pair_block = orbitals * orbitals // devices
    x_devs = 2 if freq_devs % 2 == 0 else 1
    c_devs = 2 if group_devs % 2 == 0 and per_freq % 2 == 0 else 1
    z_devs = freq_devs // x_devs
    y_devs = group_devs // c_devs
    sub = per_freq // c_devs
    freqs = z_devs * sub
    c_pos = lax.axis_index("kgrp") % c_devs

    def core_flip(values):
        return lax.ppermute(values, "kgrp", [(i, i ^ 1) for i in range(group_devs)])

    def x_flip(values):
        return lax.ppermute(values, "freq", [(i, i ^ 1) for i in range(freq_devs)])

    def z_move(values, step):
        if is_power_of_two(z_devs):
            pairs = [(i, ((i // x_devs) ^ step) * x_devs + i % x_devs) for i in range(freq_devs)]
        else:
            pairs = [
                (i, (i // x_devs + step) % z_devs * x_devs + i % x_devs) for i in range(freq_devs)
            ]
        return lax.ppermute(values, "freq", pairs)

    own = jnp.stack([self_energy, guess_factor])
    own = lax.dynamic_slice_in_dim(own, c_pos * sub, sub, 1)
    sg_blocks = [own] + [z_move(own, step) for step in range(1, z_devs)]
    near = [(hamiltonian, (0, 0))]
    far = []
    if x_devs == 2:
        crossing, _ = lax.optimization_barrier((hamiltonian, own))
        crossed = x_flip(crossing)
        crossed, sg_blocks = lax.optimization_barrier((crossed, sg_blocks))
        far.append((crossed, (1, 0)))
    if c_devs == 2:
        near += [(core_flip(block), (flip[0], 1)) for block, flip in near]
        far += [(core_flip(block), (flip[0], 1)) for block, flip in far]

    vmem = pl.BlockSpec(memory_space=pltpu.VMEM)
    smem = pl.BlockSpec(memory_space=pltpu.SMEM)
    half = orbitals // 2

    def run_kernel(first, points, extras, outputs, scratch, name):
        k_total = len(points) * k_local
        k_rows = -(-k_total // 8) * 8
        flips = tuple(flip for _, flip in points)
        sizes = (z_devs, x_devs, c_devs, sub, k_local, group_devs, freq_total, orbitals, flips)
        return pl.pallas_call(
            functools.partial(green_kernel, sizes, first),
            out_shape=outputs,
            in_specs=[smem, smem] + [vmem] * (len(points) + len(extras)),
            out_specs=jax.tree.map(lambda _: vmem, outputs),
            scratch_shapes=[
                pltpu.VMEM((k_total, freqs * orbitals, width), jnp.float32),
                pltpu.VMEM((k_rows, width), jnp.float32),
                pltpu.VMEM((k_rows, width), jnp.float32),
            ] + scratch,
            compiler_params=pltpu.CompilerParams(vmem_limit_bytes=40 * 1024 * 1024),
            name=name,
        )(weights, counts, *[block for block, _ in points], *extras)

    square = jax.ShapeDtypeStruct((freqs, orbitals, width), jnp.float32)
    shared = run_kernel(
        True,
        near,
        sg_blocks,
        (
            square,
            jax.ShapeDtypeStruct((freqs * orbitals, 2 * width), jnp.bfloat16),
            jax.ShapeDtypeStruct((freqs, 2 * width, 2 * width), jnp.bfloat16),
            square,
            jax.ShapeDtypeStruct((freqs, 8, width), jnp.float32),
        ),
        [],
        "near",
    )
    partial_sums = run_kernel(
        False,
        far,
        list(shared),
        jax.ShapeDtypeStruct((half, 2 * freqs, width), jnp.float32),
        [
            pltpu.VMEM((orbitals, width), jnp.float32),
            pltpu.VMEM((2 * freqs * half, width), jnp.float32),
        ],
        "far",
    )

    share = width // pair_block
    outgoing = partial_sums.reshape(half, 2 * freqs, share, pair_block).transpose(0, 2, 1, 3)
    outgoing = outgoing.reshape(devices, 2 * freqs, pair_block)
    arrived = lax.all_to_all(outgoing, ("freq", "kgrp"), 0, 0, tiled=True)
    result = pl.pallas_call(
        functools.partial(final_kernel, (z_devs, x_devs, y_devs, c_devs, sub)),
        out_shape=jax.ShapeDtypeStruct((2 * freq_total, pair_block), jnp.float32),
        in_specs=[vmem, vmem],
        out_specs=vmem,
        name="collect",
    )(weights.reshape(1, -1), arrived)
    return result.T


def solution(mesh):
    return jax.shard_map(
        per_device,
        mesh=mesh,
        in_specs=(
            P(("freq", "kgrp"), None, None),
            P("freq", None, None),
            P("freq", None, None),
            P(),
            P(),
        ),
        out_specs=P(("freq", "kgrp"), None),
        check_vma=False,
    )
```

time: 57.2 us -> 41.3 us (0.72); the launches traced: 56.3 us -> 41 us
  Pallas kernels: 22.1 us -> 15 us
  waiting for transfers between devices: 12 us -> 5.85 us
  blocking collectives: 12.9 us -> 11 us
    pallas_call x1 -> x2, Pallas kernels: 20.5 us -> 13.3 us  [run_kernel(): pl.pallas_call(functools.partial(green_kernel, sizes, first), out_shape=o...]
    ppermute x1, waiting for transfers between devices: 6.51 us -> 0.01 us  [x_flip(): return lax.ppermute(values, 'freq', [(i, i ^ 1) for i in range(freq_devs)])]
    all_to_all x1, blocking collectives: 12.9 us -> 11 us  [per_device(): arrived = lax.all_to_all(outgoing, ('freq', 'kgrp'), 0, 0, tiled=True)]
  transfers between devices with their start and end apart: 6 -> 6, of which waited for: 3 -> 2; matrix products, arithmetic and copies ran while one was open for 1% -> 0% of each run, Pallas kernels for 0% -> 15%
where the time goes in v2:
time: 41.3 us; the launch traced here: 41 us
  Pallas kernels  15 us (36%)
  blocking collectives  11 us (27%)
  starting transfers between devices  7.36 us (18%)
  waiting for transfers between devices  5.85 us (14%)
  local copies, waits for them, and re-layouts  0.95 us (2%)
  other arithmetic  0.81 us (2%)
    pallas_call x2, Pallas kernels, run_kernel(): pl.pallas_call(functools.partial(green_kernel, sizes, first), out_shape=o...  13.3 us
    all_to_all x1, blocking collectives, per_device(): arrived = lax.all_to_all(outgoing, ('freq', 'kgrp'), 0, 0, tiled=True)  11 us
    ppermute x3, waiting for transfers between devices, z_move(): return lax.ppermute(values, 'freq', pairs)  5.84 us
    ppermute x3, starting transfers between devices, z_move(): return lax.ppermute(values, 'freq', pairs)  4.39 us
    ppermute x1, starting transfers between devices, x_flip(): return lax.ppermute(values, 'freq', [(i, i ^ 1) for i in range(freq_devs)])  2.97 us
    pallas_call x1, Pallas kernels, per_device(): pl.pallas_call(functools.partial(final_kernel, (z_devs, x_devs, y_devs, c...  1.65 us
    unnamed x6, local copies, waits for them, and re-layouts  0.95 us
  transfers between devices with their start and end apart: 6, of which 2 were waited for; matrix products, arithmetic and copies ran while one was open for 0% of the time, Pallas kernels for 15%

profile of v2, /device:TPU:0, one launch (start us, length us, event | category | flops | bytes accessed | tf_op | source)
XLA Modules:
  0.0 41.0 jit_solution(17907933107984802496)
XLA Ops:
  0.0 0.0 copy-start.1
  0.0 0.0 copy-start.2
  0.0 0.8 %fusion.refs_2_ = f32[2,1,64,128]{3,2,1,0:T(8,128)S(1)} fusion(s32[]{:T(128)S(6)} %select_n.11, f32[1,2,64,128]{3,2,1,0:T(8,128)} %bitcast.5, f32[1,2,64,128]{3,2,1,0:T(8,128)} %bitcast.6), kind=kLoop, calls=%fused_computation.2 | loop fusion | flops 16384 | bytes 196612 | tf_op jit(solution)/shard_map/stack | solution.py:262
  0.8 3.0 %collective-permute-start = (f32[8,64,128]{2,1,0:T(8,128)}, f32[8,64,128]{2,1,0:T(8,128)S(1)}, u32[]{:S(2)}, u32[]{:S(2)}) collective-permute-start(f32[8,64,128]{2,1,0:T(8,128)} %refs_0_.1), channel_id=1, source_target_pairs={{0,4},{4,0},{8,12},{12,8},{16,20},{20,16},{24,28},{28,24},{1,5},{5... | collective-permute-start | bytes 786440 | tf_op jit(solution)/shard_map/ppermute | solution.py:251
  3.8 1.6 %collective-permute-start.1 = (f32[2,1,64,128]{3,2,1,0:T(8,128)S(1)}, f32[2,1,64,128]{3,2,1,0:T(8,128)S(1)}, u32[]{:S(2)}, u32[]{:S(2)}) collective-permute-start(f32[2,1,64,128]{3,2,1,0:T(8,128)S(1)} %fusion.refs_2_), channel_id=1, source_target_pairs={{0,8},{4,12},{8,0},{12,4},{16,24},{20,28},{24,16},{28,20},{1,9},{5... | collective-permute-start | bytes 196616 | tf_op jit(solution)/shard_map/ppermute | solution.py:260
  5.4 2.6 %collective-permute-start.2 = (f32[2,1,64,128]{3,2,1,0:T(8,128)S(1)}, f32[2,1,64,128]{3,2,1,0:T(8,128)S(1)}, u32[]{:S(2)}, u32[]{:S(2)}) collective-permute-start(f32[2,1,64,128]{3,2,1,0:T(8,128)S(1)} %fusion.refs_2_), channel_id=1, source_target_pairs={{0,16},{4,20},{8,24},{12,28},{16,0},{20,4},{24,8},{28,12},{1,17},{... | collective-permute-start | bytes 196616 | tf_op jit(solution)/shard_map/ppermute | solution.py:260
  7.9 0.2 collective-permute-start.3
  8.2 0.0 collective-permute-start.5
  8.2 0.0 collective-permute-done.1.refs_3_
  8.2 4.2 %collective-permute-done.2.refs_4_ = f32[2,1,64,128]{3,2,1,0:T(8,128)S(1)} collective-permute-done((f32[2,1,64,128]{3,2,1,0:T(8,128)S(1)}, f32[2,1,64,128]{3,2,1,0:T(8,128)S(1)}, u32[]{:S(2)}, u32[]{:S(2)}) %collective-permute-start.2) | collective-permute-done | bytes 65568 | tf_op jit(solution)/shard_map/ppermute | solution.py:260
  12.3 1.7 %collective-permute-done.3.refs_5_ = f32[2,1,64,128]{3,2,1,0:T(8,128)S(1)} collective-permute-done((f32[2,1,64,128]{3,2,1,0:T(8,128)S(1)}, f32[2,1,64,128]{3,2,1,0:T(8,128)S(1)}, u32[]{:S(2)}, u32[]{:S(2)}) %collective-permute-start.3) | collective-permute-done | bytes 65568 | tf_op jit(solution)/shard_map/ppermute | solution.py:260
  14.0 0.0 collective-permute-done.refs_0_
  14.0 0.0 collective-permute-start.4
  14.0 0.0 collective-permute-done.5.refs_1_
  14.0 0.0 copy-done.1
  14.0 0.0 copy-done.2
  14.0 0.0 copy-start
  14.1 0.9 %copy-done = f32[8,64,128]{2,1,0:T(8,128)S(1)} copy-done((f32[8,64,128]{2,1,0:T(8,128)S(1)}, f32[8,64,128]{2,1,0:T(8,128)}, u32[]{:S(2)}) %copy-start) | copy-done | bytes 262168
  15.0 6.2 %near.1 = (f32[4,64,128]{2,1,0:T(8,128)S(1)}, bf16[256,256]{1,0:T(8,128)(2,1)S(1)}, bf16[4,256,256]{2,1,0:T(8,128)(2,1)S(1)}, f32[4,64,128]{2,1,0:T(8,128)S(1)}, f32[4,8,128]{2,1,0:T(8,128)S(1)}) custom-call(s32[256]{0:T(256)S(1)} %copy-done.1, s32[16]{0:T(128)S(1)} %copy-done.2, f32[8,64,128]{2,1,0:T(8,128)S(1)} %copy-done, ...), custom_call_target="tpu_custom_call" | custom-call | tf_op jit(solution)/shard_map/near/pallas_call | solution.py:285
  21.2 0.0 collective-permute-done.4.refs_1_
  21.2 7.1 %far.1 = f32[32,8,128]{2,1,0:T(8,128)S(1)} custom-call(s32[256]{0:T(256)S(1)} %copy-done.1, s32[16]{0:T(128)S(1)} %copy-done.2, f32[8,64,128]{2,1,0:T(8,128)S(1)} %collective-permute-done.refs_0_, f32[8,64,128]{2,1,0:T(8,128)S(1)} %collective-permute-done.4.refs_1_, f32[4,64,128]{2,1,0:T(8,128)S(1)} %get-tuple-element.22.refs_2_, ...), custom_call_target="tpu_custom_call" | custom-call | tf_op jit(solution)/shard_map/far/pallas_call | solution.py:285
  28.3 11.0 %all_to_all.5.parts_ref = f32[32,8,128]{2,1,0:T(8,128)} all-to-all(f32[32,8,128]{2,1,0:T(8,128)S(1)} %far.1), channel_id=1, replica_groups=mesh['freq'=8,'kgrp'=4] {'freq','kgrp'}, dimensions={0} | all-to-all | bytes 262144 | tf_op jit(solution)/shard_map/all_to_all | solution.py:329
  39.4 1.7 %collect.1 = f32[32,128]{1,0:T(8,128)} custom-call(s32[1,256]{1,0:T(1,128)} %bitcast.4, f32[32,8,128]{2,1,0:T(8,128)} %all_to_all.5.parts_ref), custom_call_target="tpu_custom_call" | custom-call | tf_op jit(solution)/shard_map/collect/pallas_call | solution.py:330
Async XLA Ops:
  0.0 14.0 %copy-start.1 = (s32[256]{0:T(256)S(1)}, s32[256]{0:T(256)}, u32[]{:S(2)}) copy-start(s32[256]{0:T(256)} %weights_ref.3) | copy-start | bytes 3076
  0.0 14.0 %copy-start.2 = (s32[16]{0:T(128)S(1)}, s32[16]{0:T(128)}, u32[]{:S(2)}) copy-start(s32[16]{0:T(128)} %counts_ref.3) | copy-start | bytes 196
  0.8 13.2 %collective-permute-start = (f32[8,64,128]{2,1,0:T(8,128)}, f32[8,64,128]{2,1,0:T(8,128)S(1)}, u32[]{:S(2)}, u32[]{:S(2)}) collective-permute-start(f32[8,64,128]{2,1,0:T(8,128)} %refs_0_.1), channel_id=1, source_target_pairs={{0,4},{4,0},{8,12},{12,8},{16,20},{20,16},{24,28},{28,24},{1,5},{5... | collective-permute-start | bytes 786440 | tf_op jit(solution)/shard_map/ppermute | solution.py:251
  3.8 4.4 %collective-permute-start.1 = (f32[2,1,64,128]{3,2,1,0:T(8,128)S(1)}, f32[2,1,64,128]{3,2,1,0:T(8,128)S(1)}, u32[]{:S(2)}, u32[]{:S(2)}) collective-permute-start(f32[2,1,64,128]{3,2,1,0:T(8,128)S(1)} %fusion.refs_2_), channel_id=1, source_target_pairs={{0,8},{4,12},{8,0},{12,4},{16,24},{20,28},{24,16},{28,20},{1,9},{5... | collective-permute-start | bytes 196616 | tf_op jit(solution)/shard_map/ppermute | solution.py:260
  5.4 7.0 %collective-permute-start.2 = (f32[2,1,64,128]{3,2,1,0:T(8,128)S(1)}, f32[2,1,64,128]{3,2,1,0:T(8,128)S(1)}, u32[]{:S(2)}, u32[]{:S(2)}) collective-permute-start(f32[2,1,64,128]{3,2,1,0:T(8,128)S(1)} %fusion.refs_2_), channel_id=1, source_target_pairs={{0,16},{4,20},{8,24},{12,28},{16,0},{20,4},{24,8},{28,12},{1,17},{... | collective-permute-start | bytes 196616 | tf_op jit(solution)/shard_map/ppermute | solution.py:260
  7.9 6.1 %collective-permute-start.3 = (f32[2,1,64,128]{3,2,1,0:T(8,128)S(1)}, f32[2,1,64,128]{3,2,1,0:T(8,128)S(1)}, u32[]{:S(2)}, u32[]{:S(2)}) collective-permute-start(f32[2,1,64,128]{3,2,1,0:T(8,128)S(1)} %fusion.refs_2_), channel_id=1, source_target_pairs={{0,24},{4,28},{8,16},{12,20},{16,8},{20,12},{24,0},{28,4},{1,25},{... | collective-permute-start | bytes 196616 | tf_op jit(solution)/shard_map/ppermute | solution.py:260
  8.2 5.9 %collective-permute-start.5 = (f32[8,64,128]{2,1,0:T(8,128)}, f32[8,64,128]{2,1,0:T(8,128)S(1)}, u32[]{:S(2)}, u32[]{:S(2)}) collective-permute-start(f32[8,64,128]{2,1,0:T(8,128)} %refs_0_.1), channel_id=1, source_target_pairs={{0,1},{1,0},{2,3},{3,2},{4,5},{5,4},{6,7},{7,6},{8,9},{9,8},{10,11... | collective-permute-start | bytes 786440 | tf_op jit(solution)/shard_map/ppermute | solution.py:248
  14.0 7.2 %collective-permute-start.4 = (f32[8,64,128]{2,1,0:T(8,128)S(1)}, f32[8,64,128]{2,1,0:T(8,128)S(1)}, u32[]{:S(2)}, u32[]{:S(2)}) collective-permute-start(f32[8,64,128]{2,1,0:T(8,128)S(1)} %collective-permute-done.refs_0_), channel_id=1, source_target_pairs={{0,1},{1,0},{2,3},{3,2},{4,5},{5,4},{6,7},{7,6},{8,9},{9,8},{10,11... | collective-permute-start | bytes 786440 | tf_op jit(solution)/shard_map/ppermute | solution.py:248
  14.0 1.0 %copy-start = (f32[8,64,128]{2,1,0:T(8,128)S(1)}, f32[8,64,128]{2,1,0:T(8,128)}, u32[]{:S(2)}) copy-start(f32[8,64,128]{2,1,0:T(8,128)} %refs_0_.1) | copy-start | bytes 786436

commit v3 on v0

v3 whole, which is shorter than its diff:
```python
import functools
import math

import jax
import jax.numpy as jnp
from jax import lax
from jax.experimental import pallas as pl
from jax.experimental.pallas import tpu as pltpu
from jax.sharding import PartitionSpec as P


chem_potential = 0.2
BATCH = 8
COST = 400_000_000


def is_power_of_two(number):
    return number & (number - 1) == 0


def split_bf16(values):
    high = values.astype(jnp.bfloat16)
    low = (values - high.astype(jnp.float32)).astype(jnp.bfloat16)
    return high, low


def swap_halves(values):
    return pltpu.roll(values, values.shape[-1] // 2, 1)


def block_form(values, swap_sign):
    return jnp.concatenate([values, swap_halves(values) * swap_sign], 0)


def left_tile(high, low):
    return jnp.concatenate([high, low], -1)


def right_tile(high, low):
    upper = jnp.concatenate([high, low], -1)
    lower = jnp.concatenate([high, jnp.zeros_like(low)], -1)
    return jnp.concatenate([upper, lower], 0)


def add_halves(both):
    width = both.shape[-1] // 2
    return both[:, :width] + both[:, width:]


def product(left, right):
    return add_halves(jnp.dot(left, right, preferred_element_type=jnp.float32))


class Layout:
    def __init__(self, hamiltonian, self_energy):
        self.k_local, self.orbitals, self.width = hamiltonian.shape
        per_freq = self_energy.shape[0]
        self.freq_devs = lax.axis_size("freq")
        self.group_devs = lax.axis_size("kgrp")
        self.freq_total = per_freq * self.freq_devs
        self.x_devs = 2 if self.freq_devs % 2 == 0 else 1
        self.c_devs = 2 if self.group_devs % 2 == 0 and per_freq % 2 == 0 else 1
        self.z_devs = self.freq_devs // self.x_devs
        self.y_devs = self.group_devs // self.c_devs
        self.sub = per_freq // self.c_devs
        self.freqs = self.z_devs * self.sub

    def positions(self):
        freq_pos = lax.axis_index("freq")
        group_pos = lax.axis_index("kgrp")
        return freq_pos, group_pos, group_pos % self.c_devs

    def block_of(self, step):
        z_pos = lax.axis_index("freq") // self.x_devs
        if is_power_of_two(self.z_devs):
            return z_pos ^ step
        return (z_pos + self.z_devs - step) % self.z_devs

    def freq_of(self, place):
        freq_pos, _, c_pos = self.positions()
        block = self.block_of(place // self.sub) * self.x_devs + freq_pos % self.x_devs
        return block * (self.c_devs * self.sub) + c_pos * self.sub + place % self.sub

    def matsubara(self, place):
        return (2 * self.freq_of(place) + 1).astype(jnp.float32) * (math.pi / (2 * self.freq_total))

    def plane_of(self, place):
        return self.block_of(place // self.sub) * self.sub + place % self.sub


class Masks:
    def __init__(self, orbitals):
        width = 2 * orbitals
        row = lax.broadcasted_iota(jnp.int32, (orbitals, width), 0)
        lane = lax.broadcasted_iota(jnp.int32, (orbitals, width), 1)
        self.eye_left = (lane == row).astype(jnp.float32)
        self.eye_right = (lane == row + orbitals).astype(jnp.float32)
        self.eye_both = self.eye_left + self.eye_right
        self.eye_block = jnp.concatenate([self.eye_left, self.eye_right], 0)
        self.left_row = lax.broadcasted_iota(jnp.int32, (1, width), 1) < orbitals
        self.sign = jnp.where(self.left_row, -1.0, 1.0)


def prepare_frequency(plan, masks, place, sigma, guess, target, left_ref, right_ref, shift_ref, rows_ref):
    orbitals = plan.orbitals
    matsubara = plan.matsubara(place)
    high, low = split_bf16(block_form(guess, masks.sign))
    left = left_tile(high[:orbitals], low[:orbitals])
    left_ref[pl.ds(target * orbitals, orbitals), :] = left
    right_ref[target] = left_tile(high, low)
    energy = masks.eye_left * chem_potential + masks.eye_right * matsubara
    matrix = split_bf16(block_form(energy - sigma, masks.sign))
    shift_ref[target] = product(left, right_tile(*matrix))
    sigma_diag = jnp.sum(sigma * masks.eye_both, 0, keepdims=True)
    sigma_swap = swap_halves(sigma_diag)
    real = chem_potential - jnp.where(masks.left_row, sigma_diag, sigma_swap)
    imag = matsubara - jnp.where(masks.left_row, sigma_swap, sigma_diag)
    rows_ref[target, pl.ds(0, 1), :] = real
    rows_ref[target, pl.ds(1, 1), :] = imag


def diagonal_row(masks, matrix):
    diag = jnp.sum(matrix * masks.eye_left, 0, keepdims=True)
    return diag + swap_halves(diag)


def sum_points(plan, masks, rows, constant, load_t, diags, weights, total):
    orbitals = plan.orbitals
    real = rows[0:1] - diags
    imag = jnp.broadcast_to(rows[1:2], real.shape)
    modulus = real * real + imag * imag
    d_real = real / modulus
    d_imag = -imag / modulus
    d_start = jnp.where(masks.left_row, d_real, d_imag) * weights
    d_turned = d_imag * masks.sign
    d_signed = d_real * masks.sign

    def errors_of(items):
        errors = []
        for item in items:
            mixed = constant - load_t(item)
            turned = swap_halves(mixed)
            upper = mixed * d_real[item:item + 1] + turned * d_turned[item:item + 1]
            lower = turned * d_signed[item:item + 1] - mixed * d_imag[item:item + 1]
            errors.append(split_bf16(masks.eye_block - jnp.concatenate([upper, lower], 0)))
        return errors

    def advance(series, powers):
        next_series, next_powers = [], []
        for start, (high, low) in zip(series, powers):
            s_high, s_low = split_bf16(start)
            stacked = jnp.concatenate([left_tile(s_high, s_low), left_tile(high[:orbitals], low[:orbitals])], 0)
            both = product(stacked, right_tile(high, low))
            next_series.append(start + both[:orbitals])
            next_powers.append(split_bf16(block_form(both[orbitals:], masks.sign)))
        return next_series, next_powers

    def finish(total, series, powers):
        lefts = [left_tile(*split_bf16(start)) for start in series]
        rights = [right_tile(*power) for power in powers]
        for start in series:
            total = total + start
        return total + product(jnp.concatenate(lefts, 1), jnp.concatenate(rights, 0))

    def accumulate(advances, total):
        for begin in range(0, plan.k_total, BATCH):
            items = range(begin, min(begin + BATCH, plan.k_total))
            series = [masks.eye_both * d_start[item:item + 1] for item in items]
            powers = errors_of(items)
            for _ in range(advances):
                series, powers = advance(series, powers)
            total = finish(total, series, powers)
        return total

    return lambda advances: accumulate(advances, total)


def run_counts(count, accumulate, store):
    @pl.when(count <= 1)
    def _():
        store(accumulate(0))

    @pl.when(count == 2)
    def _():
        store(accumulate(1))

    @pl.when(count >= 3)
    def _():
        store(accumulate(2))


def first_kernel(plan, flips, weights_ref, counts_ref, sg_ref, *refs):
    k_local, orbitals = plan.k_local, plan.orbitals
    near = len(flips[0])
    h_refs, refs = refs[:near], refs[near:]
    sum_ref, left_ref, right_ref, shift_ref, rows_ref, hs_ref, hd_ref, wr_ref, t_ref = refs
    masks = Masks(orbitals)
    freq_pos, group_pos, _ = plan.positions()
    for place in range(plan.sub):
        prepare_frequency(
            plan, masks, place, sg_ref[0, place], sg_ref[1, place], place,
            left_ref, right_ref, shift_ref, rows_ref,
        )
    for group, members in enumerate(flips):
        for piece, (x_flip, c_flip) in enumerate(members):
            first_k = ((freq_pos ^ x_flip) * plan.group_devs + (group_pos ^ c_flip)) * k_local
            for local in range(k_local):
                weight = weights_ref[first_k + local].astype(jnp.float32)
                place = piece * k_local + local
                wr_ref[group, pl.ds(place, 1), :] = jnp.full((1, plan.width), weight, jnp.float32)
    for piece in range(near):
        for local in range(k_local):
            place = piece * k_local + local
            matrix = h_refs[piece][local]
            high, low = split_bf16(block_form(matrix, masks.sign))
            hs_ref[place] = left_tile(high, low)
            hd_ref[pl.ds(place, 1), :] = diagonal_row(masks, matrix)
            t_ref[place] = product(left_ref[...], right_tile(high, low))

    def one_frequency(place, carry):
        offset = pl.multiple_of(place * orbitals, orbitals)

        def store(total):
            sum_ref[place] = total

        accumulate = sum_points(
            plan, masks, rows_ref[place], shift_ref[place],
            lambda item: t_ref[item, pl.ds(offset, orbitals), :],
            hd_ref[...], wr_ref[0], jnp.zeros((orbitals, plan.width), jnp.float32),
        )
        run_counts(counts_ref[plan.freq_of(place)], accumulate, store)
        return carry

    lax.fori_loop(0, plan.sub, one_frequency, 0)


def near_kernel(plan, counts_ref, *refs):
    orbitals, width, sub = plan.orbitals, plan.width, plan.sub
    steps = plan.z_devs - 1
    sg_refs, refs = refs[:steps], refs[steps:]
    old_refs, refs = refs[:5], refs[5:]
    hs_ref, hd_ref, wr_ref = refs[:3]
    new_refs, (t_ref,) = refs[3:8], refs[8:]
    sum_ref, left_ref, right_ref, shift_ref, rows_ref = new_refs
    masks = Masks(orbitals)
    left_ref[pl.ds(0, sub * orbitals), :] = old_refs[1][...]
    for old_ref, new_ref in zip(old_refs, new_refs):
        if old_ref is not old_refs[1]:
            for place in range(sub):
                new_ref[place] = old_ref[place]
    for place in range(sub, plan.freqs):
        sg_ref = sg_refs[place // sub - 1]
        prepare_frequency(
            plan, masks, place, sg_ref[0, place % sub], sg_ref[1, place % sub], place,
            left_ref, right_ref, shift_ref, rows_ref,
        )
    lefts = left_ref[pl.ds(sub * orbitals, (plan.freqs - sub) * orbitals), :]
    for item in range(plan.k_total):
        tile = hs_ref[item]
        t_ref[item] = product(lefts, right_tile(tile[:, :width], tile[:, width:]))

    def one_frequency(place, carry):
        offset = pl.multiple_of((place - sub) * orbitals, orbitals)

        def store(total):
            sum_ref[place] = total

        accumulate = sum_points(
            plan, masks, rows_ref[place], shift_ref[place],
            lambda item: t_ref[item, pl.ds(offset, orbitals), :],
            hd_ref[...], wr_ref[0], jnp.zeros((orbitals, width), jnp.float32),
        )
        run_counts(counts_ref[plan.freq_of(place)], accumulate, store)
        return carry

    lax.fori_loop(sub, plan.freqs, one_frequency, 0)


def far_kernel(plan, group, pieces, counts_ref, *refs):
    k_local, orbitals, width, freqs = plan.k_local, plan.orbitals, plan.width, plan.freqs
    half = orbitals // 2
    h_refs, refs = refs[:pieces], refs[pieces:]
    old_ref, left_ref, right_ref, shift_ref, rows_ref, wr_ref = refs[:6]
    out_ref, t_ref, hd_ref, r_ref, plane_ref = refs[6:]
    masks = Masks(orbitals)
    for piece in range(pieces):
        for local in range(k_local):
            place = piece * k_local + local
            matrix = h_refs[piece][local]
            hd_ref[pl.ds(place, 1), :] = diagonal_row(masks, matrix)
            tile = right_tile(*split_bf16(block_form(matrix, masks.sign)))
            t_ref[place] = product(left_ref[...], tile)

    def one_frequency(place, carry):
        offset = pl.multiple_of(place * orbitals, orbitals)

        def store(total):
            tile = right_ref[place]
            right = right_tile(tile[:, :width], tile[:, width:])
            r_ref[...] = product(left_tile(*split_bf16(total)), right)

        if pieces:
            accumulate = sum_points(
                plan, masks, rows_ref[place], shift_ref[place],
                lambda item: t_ref[item, pl.ds(offset, orbitals), :],
                hd_ref[...], wr_ref[group], old_ref[place],
            )
            run_counts(counts_ref[plan.freq_of(place)], accumulate, store)
        else:
            store(old_ref[place])
        even = r_ref[pl.ds(0, half, stride=2), :]
        odd = r_ref[pl.ds(1, half, stride=2), :]
        plane = plan.plane_of(place)
        real_rows = pl.multiple_of(plane * half, half)
        imag_rows = pl.multiple_of((freqs + plane) * half, half)
        plane_ref[pl.ds(real_rows, half), :] = jnp.where(masks.left_row, even, swap_halves(odd))
        plane_ref[pl.ds(imag_rows, half), :] = jnp.where(masks.left_row, swap_halves(even), odd)
        return carry

    lax.fori_loop(0, freqs, one_frequency, 0)
    for line in range(half):
        out_ref[line] = plane_ref[pl.ds(line, 2 * freqs, stride=half), :]


def final_kernel(sizes, weights_ref, parts_ref, out_ref):
    z_devs, x_devs, y_devs, c_devs, sub = sizes
    total = jnp.sum(weights_ref[...].astype(jnp.float32))
    shared = x_devs * c_devs
    for x_pos in range(x_devs):
        for c_pos in range(c_devs):
            gathered = None
            for z_pos in range(z_devs):
                for y_pos in range(y_devs):
                    source = ((z_pos * x_devs + x_pos) * y_devs + y_pos) * c_devs + c_pos
                    part = parts_ref[source]
                    gathered = part if gathered is None else gathered + part
            gathered = gathered / total
            place = x_pos * c_devs + c_pos
            if sub == 1:
                out_ref[pl.ds(place, 2 * z_devs, stride=shared), :] = gathered
            else:
                for group in range(2 * z_devs):
                    out_ref[pl.ds((group * shared + place) * sub, sub), :] = gathered[
                        group * sub:(group + 1) * sub
                    ]


def local_green(hamiltonian, self_energy, guess_factor, weights, counts):
    plan = Layout(hamiltonian, self_energy)
    orbitals, width, sub, freqs = plan.orbitals, plan.width, plan.sub, plan.freqs
    x_devs, z_devs, k_local = plan.x_devs, plan.z_devs, plan.k_local
    devices = plan.freq_devs * plan.group_devs
    pair_block = orbitals * orbitals // devices
    half = orbitals // 2
    c_pos = plan.positions()[2]

    def core_flip(values):
        return lax.ppermute(values, "kgrp", [(i, i ^ 1) for i in range(plan.group_devs)])

    def x_flip(values):
        return lax.ppermute(values, "freq", [(i, i ^ 1) for i in range(plan.freq_devs)])

    def z_move(values, step):
        pairs = []
        for i in range(plan.freq_devs):
            z_pos, x_pos = i // x_devs, i % x_devs
            target = z_pos ^ step if is_power_of_two(z_devs) else (z_pos + step) % z_devs
            pairs.append((i, target * x_devs + x_pos))
        return lax.ppermute(values, "freq", pairs)

    own = jnp.stack([self_energy, guess_factor])
    own = lax.dynamic_slice_in_dim(own, c_pos * sub, sub, 1)
    others = [z_move(own, step) for step in range(1, z_devs)]
    near, near_flips, far, far_flips = [hamiltonian], [(0, 0)], [], []
    if plan.c_devs == 2:
        near.append(core_flip(hamiltonian))
        near_flips.append((0, 1))
    if x_devs == 2:
        crossing, _ = lax.optimization_barrier((hamiltonian, own))
        far.append(x_flip(crossing))
        far_flips.append((1, 0))
        if plan.c_devs == 2:
            far_flips.append((1, 1))
    flips = (tuple(near_flips), tuple(far_flips))
    plan.k_total = len(near) * k_local
    k_rows = -(-plan.k_total // 8) * 8

    vmem = pl.BlockSpec(memory_space=pltpu.VMEM)
    smem = pl.BlockSpec(memory_space=pltpu.SMEM)
    params = pltpu.CompilerParams(vmem_limit_bytes=40 * 1024 * 1024)

    estimate = pl.CostEstimate(flops=COST, bytes_accessed=1 << 20, transcendentals=0)

    def f32(*shape):
        return jax.ShapeDtypeStruct(shape, jnp.float32)

    def bf16(*shape):
        return jax.ShapeDtypeStruct(shape, jnp.bfloat16)

    def shared(places):
        return [
            f32(places, orbitals, width),
            bf16(places * orbitals, 2 * width),
            bf16(places, 2 * orbitals, 2 * width),
            f32(places, orbitals, width),
            f32(places, 8, width),
        ]

    outputs = shared(sub) + [
        bf16(plan.k_total, 2 * orbitals, 2 * width), f32(k_rows, width), f32(2, k_rows, width)
    ]
    lead = pl.pallas_call(
        functools.partial(first_kernel, plan, flips),
        out_shape=outputs,
        in_specs=[smem, smem] + [vmem] * (1 + len(near)),
        out_specs=[vmem] * len(outputs),
        scratch_shapes=[pltpu.VMEM((plan.k_total, sub * orbitals, width), jnp.float32)],
        compiler_params=params,
        cost_estimate=estimate,
        name="first",
    )
    *old, h_tiles, h_diags, w_rows = lead(weights, counts, own, *near)
    outputs = shared(freqs)
    shares = pl.pallas_call(
        functools.partial(near_kernel, plan),
        out_shape=outputs,
        in_specs=[smem] + [vmem] * (len(others) + len(old) + 3),
        out_specs=[vmem] * len(outputs),
        scratch_shapes=[pltpu.VMEM((plan.k_total, (freqs - sub) * orbitals, width), jnp.float32)],
        compiler_params=params,
        cost_estimate=estimate,
        name="near",
    )(counts, *others, *old, h_tiles, h_diags, w_rows)
    if far and plan.c_devs == 2:
        crossed, _ = lax.optimization_barrier((far[0], w_rows))
        far.append(core_flip(crossed))
    partial_sums = pl.pallas_call(
        functools.partial(far_kernel, plan, 1, len(far)),
        out_shape=f32(half, 2 * freqs, width),
        in_specs=[smem] + [vmem] * (len(far) + len(shares) + 1),
        out_specs=vmem,
        scratch_shapes=[
            pltpu.VMEM((plan.k_total, freqs * orbitals, width), jnp.float32),
            pltpu.VMEM((k_rows, width), jnp.float32),
            pltpu.VMEM((orbitals, width), jnp.float32),
            pltpu.VMEM((2 * freqs * half, width), jnp.float32),
        ],
        compiler_params=params,
        name="far",
    )(counts, *far, *shares, w_rows)

    share = width // pair_block
    outgoing = partial_sums.reshape(half, 2 * freqs, share, pair_block).transpose(0, 2, 1, 3)
    outgoing = outgoing.reshape(devices, 2 * freqs, pair_block)
    arrived = lax.all_to_all(outgoing, ("freq", "kgrp"), 0, 0, tiled=True)
    result = pl.pallas_call(
        functools.partial(final_kernel, (z_devs, x_devs, plan.y_devs, plan.c_devs, sub)),
        out_shape=f32(2 * plan.freq_total, pair_block),
        in_specs=[vmem, vmem],
        out_specs=vmem,
        name="collect",
    )(weights.reshape(1, -1), arrived)
    return result.T


def solution(mesh):
    return jax.shard_map(
        local_green,
        mesh=mesh,
        in_specs=(
            P(("freq", "kgrp"), None, None),
            P("freq", None, None),
            P("freq", None, None),
            P(),
            P(),
        ),
        out_specs=P(("freq", "kgrp"), None),
        check_vma=False,
    )
```

time: 255 us -> 45.1 us (0.18)
  matrix products: 74.9 us -> 0 us
  waiting for transfers between devices: 70.5 us -> 9.54 us
  other arithmetic: 44.8 us -> 0.81 us
  local copies, waits for them, and re-layouts: 42.3 us -> 0.97 us
  between operations: 13.6 us -> 0.05 us
  blocking collectives: 0 us -> 13.1 us
  Pallas kernels: 0 us -> 13 us
  loops' own time: 3.03 us -> 0 us
    dot_general x7 -> x0, matrix products: 74.9 us -> none  [the longest x6 62.6 us: complex_product(): jnp.einsum('...ij,...jl->...il', left_side, blockify(right_side), precisi...]
    all_gather x1 -> x0, waiting for transfers between devices: 46.8 us -> none  [per_device(): h_piece = lax.all_gather(hamiltonian, 'freq', axis=0, tiled=True)]
    sub x2 -> x0, other arithmetic: 24.6 us -> none  [the longest x1 22.3 us: build_matrix(): return diagonal_shift[:, None] - kpoint_rows[None] - sigma_rows[:, None]]
    reduce_scatter x1 -> x0, waiting for transfers between devices: 16.9 us -> none  [per_device(): lax.psum_scatter(partial_term, 'kgrp', scatter_dimension=3, tiled=True)]
    neg x6 -> x0, other arithmetic: 14.8 us -> none  [blockify(): lower_row = jnp.concatenate([-imag_part, real_part], -1)]
    all_to_all x0 -> x1, blocking collectives: none -> 13.1 us  [local_green(): arrived = lax.all_to_all(outgoing, ('freq', 'kgrp'), 0, 0, tiled=True)]
    pallas_call x0 -> x4, Pallas kernels: none -> 13 us  [the longest x1 5.57 us: local_green(): pl.pallas_call(functools.partial(far_kernel, plan, 1, len(far)), out_shap...]
    ppermute x0 -> x6, waiting for transfers between devices: none -> 9.54 us  [the longest x3 6.06 us: z_move(): return lax.ppermute(values, 'freq', pairs)]
  transfers between devices with their start and end apart: 3 -> 6, of which waited for: 3 -> 4; matrix products, arithmetic and copies ran while one was open for 3% -> 2% of each run, Pallas kernels for 0% -> 13%
where the time goes in v3:
time: 45.1 us; the launch traced here: 44.8 us
  blocking collectives  13.1 us (29%)
  Pallas kernels  13 us (29%)
  waiting for transfers between devices  9.54 us (21%)
  starting transfers between devices  7.39 us (16%)
  local copies, waits for them, and re-layouts  0.97 us (2%)
  other arithmetic  0.81 us (2%)
    all_to_all x1, blocking collectives, local_green(): arrived = lax.all_to_all(outgoing, ('freq', 'kgrp'), 0, 0, tiled=True)  13.1 us
    ppermute x3, waiting for transfers between devices, z_move(): return lax.ppermute(values, 'freq', pairs)  6.06 us
    pallas_call x1, Pallas kernels, local_green(): pl.pallas_call(functools.partial(far_kernel, plan, 1, len(far)), out_shap...  5.57 us
    ppermute x3, starting transfers between devices, z_move(): return lax.ppermute(values, 'freq', pairs)  4.42 us
    ppermute x1, waiting for transfers between devices, x_flip(): lax.ppermute(values, 'freq', [(i, i ^ 1) for i in range(plan.freq_devs)])  3.47 us
    pallas_call x1, Pallas kernels, local_green(): pl.pallas_call(functools.partial(near_kernel, plan), out_shape=outputs, i...  3.03 us
    pallas_call x1, Pallas kernels, local_green(): *old, h_tiles, h_diags, w_rows = lead(weights, counts, own, *near)  2.72 us
    ppermute x1, starting transfers between devices, x_flip(): lax.ppermute(values, 'freq', [(i, i ^ 1) for i in range(plan.freq_devs)])  2.48 us
  transfers between devices with their start and end apart: 6, of which 4 were waited for; matrix products, arithmetic and copies ran while one was open for 2% of the time, Pallas kernels for 13%

profile of v3, /device:TPU:0, one launch (start us, length us, event | category | flops | bytes accessed | tf_op | source)
XLA Modules:
  0.0 44.8 jit_solution(6286173603864554130)
XLA Ops:
  0.0 0.5 %collective-permute-start.1 = (f32[8,64,128]{2,1,0:T(8,128)}, f32[8,64,128]{2,1,0:T(8,128)S(1)}, u32[]{:S(2)}, u32[]{:S(2)}) collective-permute-start(f32[8,64,128]{2,1,0:T(8,128)} %refs_0_.1), channel_id=1, source_target_pairs={{0,1},{1,0},{2,3},{3,2},{4,5},{5,4},{6,7},{7,6},{8,9},{9,8},{10,11... | collective-permute-start | bytes 786440 | tf_op jit(solution)/shard_map/ppermute | solution.py:358
  0.5 0.0 copy-start
  0.5 0.0 copy-start.1
  0.5 0.8 %fusion.sg_ref = f32[2,1,64,128]{3,2,1,0:T(8,128)S(1)} fusion(s32[]{:T(128)S(6)} %select_n.11, f32[1,2,64,128]{3,2,1,0:T(8,128)} %bitcast.5, f32[1,2,64,128]{3,2,1,0:T(8,128)} %bitcast.6), kind=kLoop, calls=%fused_computation.2 | loop fusion | flops 16384 | bytes 196612 | tf_op jit(solution)/shard_map/stack | solution.py:371
  1.3 2.5 %collective-permute-start = (f32[8,64,128]{2,1,0:T(8,128)}, f32[8,64,128]{2,1,0:T(8,128)S(1)}, u32[]{:S(2)}, u32[]{:S(2)}) collective-permute-start(f32[8,64,128]{2,1,0:T(8,128)} %refs_0_.1), channel_id=1, source_target_pairs={{0,4},{4,0},{8,12},{12,8},{16,20},{20,16},{24,28},{28,24},{1,5},{5... | collective-permute-start | bytes 786440 | tf_op jit(solution)/shard_map/ppermute | solution.py:361
  3.8 0.0 collective-permute-done.1.refs_1_
  3.8 0.0 copy-done
  3.8 0.0 copy-done.1
  3.8 0.0 copy-start.2
  3.8 1.0 %copy-done.2 = f32[8,64,128]{2,1,0:T(8,128)S(1)} copy-done((f32[8,64,128]{2,1,0:T(8,128)S(1)}, f32[8,64,128]{2,1,0:T(8,128)}, u32[]{:S(2)}) %copy-start.2) | copy-done | bytes 262168
  4.8 2.7 %first.1 = (f32[1,64,128]{2,1,0:T(8,128)S(1)}, bf16[64,256]{1,0:T(8,128)(2,1)S(1)}, bf16[1,128,256]{2,1,0:T(8,128)(2,1)S(1)}, f32[1,64,128]{2,1,0:T(8,128)S(1)},...) custom-call(s32[256]{0:T(256)S(1)} %copy-done, ...), custom_call_target="tpu_custom_call" | custom-call | flops 400000000 | bytes 1048576 | tf_op jit(solution)/shard_map/first/pallas_call | solution.py:422
  7.5 3.5 %collective-permute-done.refs_0_ = f32[8,64,128]{2,1,0:T(8,128)S(1)} collective-permute-done((f32[8,64,128]{2,1,0:T(8,128)}, f32[8,64,128]{2,1,0:T(8,128)S(1)}, u32[]{:S(2)}, u32[]{:S(2)}) %collective-permute-start) | collective-permute-done | bytes 262176 | tf_op jit(solution)/shard_map/ppermute | solution.py:361
  11.0 0.0 collective-permute-start.2
  11.0 1.8 %collective-permute-start.3 = (f32[2,1,64,128]{3,2,1,0:T(8,128)S(1)}, f32[2,1,64,128]{3,2,1,0:T(8,128)S(1)}, u32[]{:S(2)}, u32[]{:S(2)}) collective-permute-start(f32[2,1,64,128]{3,2,1,0:T(8,128)S(1)} %fusion.sg_ref), channel_id=1, source_target_pairs={{0,8},{4,12},{8,0},{12,4},{16,24},{20,28},{24,16},{28,20},{1,9},{5... | collective-permute-start | bytes 196616 | tf_op jit(solution)/shard_map/ppermute | solution.py:369
  12.8 2.6 %collective-permute-start.4 = (f32[2,1,64,128]{3,2,1,0:T(8,128)S(1)}, f32[2,1,64,128]{3,2,1,0:T(8,128)S(1)}, u32[]{:S(2)}, u32[]{:S(2)}) collective-permute-start(f32[2,1,64,128]{3,2,1,0:T(8,128)S(1)} %fusion.sg_ref), channel_id=1, source_target_pairs={{0,16},{4,20},{8,24},{12,28},{16,0},{20,4},{24,8},{28,12},{1,17},{... | collective-permute-start | bytes 196616 | tf_op jit(solution)/shard_map/ppermute | solution.py:369
  15.4 0.0 collective-permute-start.5
  15.4 0.2 collective-permute-done.3.refs_0_
  15.6 4.2 %collective-permute-done.4.refs_1_ = f32[2,1,64,128]{3,2,1,0:T(8,128)S(1)} collective-permute-done((f32[2,1,64,128]{3,2,1,0:T(8,128)S(1)}, f32[2,1,64,128]{3,2,1,0:T(8,128)S(1)}, u32[]{:S(2)}, u32[]{:S(2)}) %collective-permute-start.4) | collective-permute-done | bytes 65568 | tf_op jit(solution)/shard_map/ppermute | solution.py:369
  19.8 1.7 %collective-permute-done.5.refs_2_ = f32[2,1,64,128]{3,2,1,0:T(8,128)S(1)} collective-permute-done((f32[2,1,64,128]{3,2,1,0:T(8,128)S(1)}, f32[2,1,64,128]{3,2,1,0:T(8,128)S(1)}, u32[]{:S(2)}, u32[]{:S(2)}) %collective-permute-start.5) | collective-permute-done | bytes 65568 | tf_op jit(solution)/shard_map/ppermute | solution.py:369
  21.5 3.0 %near.1 = (f32[4,64,128]{2,1,0:T(8,128)S(1)}, bf16[256,256]{1,0:T(8,128)(2,1)S(1)}, bf16[4,128,256]{2,1,0:T(8,128)(2,1)S(1)}, f32[4,64,128]{2,1,0:T(8,128)S(1)}, f32[4,8,128]{2,1,0:T(8,128)S(1)}) custom-call(s32[16]{0:T(128)S(1)} %copy-done.1, f32[2,1,64,128]{3,2,1,0:T(8,128)S(1)} %collective-permute-done.3.refs_0_, ...), custom_call_target="tpu_custom_call" | custom-call | flops 400000000 | bytes 1048576 | tf_op jit(solution)/shard_map/near/pallas_call | solution.py:424
  24.5 0.0 collective-permute-done.2.refs_1_
  24.5 5.6 %far.1 = f32[32,8,128]{2,1,0:T(8,128)S(1)} custom-call(s32[16]{0:T(128)S(1)} %copy-done.1, f32[8,64,128]{2,1,0:T(8,128)S(1)} %collective-permute-done.refs_0_, f32[8,64,128]{2,1,0:T(8,128)S(1)} %collective-permute-done.2.refs_1_, f32[4,64,128]{2,1,0:T(8,128)S(1)} %get-tuple-element.30.refs_2_, bf16[256,256]{1,0:T(8,128)(2,1)S(1)} %get-tuple-element.31.refs_3_, ...), custom_call_target="tpu_custom_call" | custom-call | tf_op jit(solution)/shard_map/far/pallas_call | solution.py:437
  30.1 13.1 %all_to_all.5.parts_ref = f32[32,8,128]{2,1,0:T(8,128)} all-to-all(f32[32,8,128]{2,1,0:T(8,128)S(1)} %far.1), channel_id=1, replica_groups=mesh['freq'=8,'kgrp'=4] {'freq','kgrp'}, dimensions={0} | all-to-all | bytes 262144 | tf_op jit(solution)/shard_map/all_to_all | solution.py:455
  43.2 1.7 %collect.1 = f32[32,128]{1,0:T(8,128)} custom-call(s32[1,256]{1,0:T(1,128)} %bitcast.4, f32[32,8,128]{2,1,0:T(8,128)} %all_to_all.5.parts_ref), custom_call_target="tpu_custom_call" | custom-call | tf_op jit(solution)/shard_map/collect/pallas_call | solution.py:456
Async XLA Ops:
  0.0 3.8 %collective-permute-start.1 = (f32[8,64,128]{2,1,0:T(8,128)}, f32[8,64,128]{2,1,0:T(8,128)S(1)}, u32[]{:S(2)}, u32[]{:S(2)}) collective-permute-start(f32[8,64,128]{2,1,0:T(8,128)} %refs_0_.1), channel_id=1, source_target_pairs={{0,1},{1,0},{2,3},{3,2},{4,5},{5,4},{6,7},{7,6},{8,9},{9,8},{10,11... | collective-permute-start | bytes 786440 | tf_op jit(solution)/shard_map/ppermute | solution.py:358
  0.5 3.3 %copy-start = (s32[256]{0:T(256)S(1)}, s32[256]{0:T(256)}, u32[]{:S(2)}) copy-start(s32[256]{0:T(256)} %weights_ref.1) | copy-start | bytes 3076
  0.5 3.3 %copy-start.1 = (s32[16]{0:T(128)S(1)}, s32[16]{0:T(128)}, u32[]{:S(2)}) copy-start(s32[16]{0:T(128)} %counts_ref.5) | copy-start | bytes 196
  1.3 9.7 %collective-permute-start = (f32[8,64,128]{2,1,0:T(8,128)}, f32[8,64,128]{2,1,0:T(8,128)S(1)}, u32[]{:S(2)}, u32[]{:S(2)}) collective-permute-start(f32[8,64,128]{2,1,0:T(8,128)} %refs_0_.1), channel_id=1, source_target_pairs={{0,4},{4,0},{8,12},{12,8},{16,20},{20,16},{24,28},{28,24},{1,5},{5... | collective-permute-start | bytes 786440 | tf_op jit(solution)/shard_map/ppermute | solution.py:361
  3.8 1.0 %copy-start.2 = (f32[8,64,128]{2,1,0:T(8,128)S(1)}, f32[8,64,128]{2,1,0:T(8,128)}, u32[]{:S(2)}) copy-start(f32[8,64,128]{2,1,0:T(8,128)} %refs_0_.1) | copy-start | bytes 786436
  11.0 13.5 %collective-permute-start.2 = (f32[8,64,128]{2,1,0:T(8,128)S(1)}, f32[8,64,128]{2,1,0:T(8,128)S(1)}, u32[]{:S(2)}, u32[]{:S(2)}) collective-permute-start(f32[8,64,128]{2,1,0:T(8,128)S(1)} %collective-permute-done.refs_0_), channel_id=1, source_target_pairs={{0,1},{1,0},{2,3},{3,2},{4,5},{5,4},{6,7},{7,6},{8,9},{9,8},{10,11... | collective-permute-start | bytes 786440 | tf_op jit(solution)/shard_map/ppermute | solution.py:358
  11.0 4.6 %collective-permute-start.3 = (f32[2,1,64,128]{3,2,1,0:T(8,128)S(1)}, f32[2,1,64,128]{3,2,1,0:T(8,128)S(1)}, u32[]{:S(2)}, u32[]{:S(2)}) collective-permute-start(f32[2,1,64,128]{3,2,1,0:T(8,128)S(1)} %fusion.sg_ref), channel_id=1, source_target_pairs={{0,8},{4,12},{8,0},{12,4},{16,24},{20,28},{24,16},{28,20},{1,9},{5... | collective-permute-start | bytes 196616 | tf_op jit(solution)/shard_map/ppermute | solution.py:369
  12.8 7.0 %collective-permute-start.4 = (f32[2,1,64,128]{3,2,1,0:T(8,128)S(1)}, f32[2,1,64,128]{3,2,1,0:T(8,128)S(1)}, u32[]{:S(2)}, u32[]{:S(2)}) collective-permute-start(f32[2,1,64,128]{3,2,1,0:T(8,128)S(1)} %fusion.sg_ref), channel_id=1, source_target_pairs={{0,16},{4,20},{8,24},{12,28},{16,0},{20,4},{24,8},{28,12},{1,17},{... | collective-permute-start | bytes 196616 | tf_op jit(solution)/shard_map/ppermute | solution.py:369
  15.4 6.1 %collective-permute-start.5 = (f32[2,1,64,128]{3,2,1,0:T(8,128)S(1)}, f32[2,1,64,128]{3,2,1,0:T(8,128)S(1)}, u32[]{:S(2)}, u32[]{:S(2)}) collective-permute-start(f32[2,1,64,128]{3,2,1,0:T(8,128)S(1)} %fusion.sg_ref), channel_id=1, source_target_pairs={{0,24},{4,28},{8,16},{12,20},{16,8},{20,12},{24,0},{28,4},{1,25},{... | collective-permute-start | bytes 196616 | tf_op jit(solution)/shard_map/ppermute | solution.py:369

commit v4 on v3

--- a/solution.py
+++ b/solution.py
@@ -64,6 +64,8 @@
         self.y_devs = self.group_devs // self.c_devs
         self.sub = per_freq // self.c_devs
         self.freqs = self.z_devs * self.sub
+        self.lead_steps = min(2, self.z_devs)
+        self.lead = self.lead_steps * self.sub
 
     def positions(self):
         freq_pos = lax.axis_index("freq")
@@ -189,33 +191,54 @@
         store(accumulate(2))
 
 
-def first_kernel(plan, flips, weights_ref, counts_ref, sg_ref, *refs):
+def fetch(source_ref, target_ref, semaphore):
+    copy = pltpu.make_async_copy(source_ref, target_ref, semaphore)
+    copy.start()
+    return copy
+
+
+def first_kernel(plan, flips, weights_ref, counts_ref, own_ref, *refs):
     k_local, orbitals = plan.k_local, plan.orbitals
-    near = len(flips[0])
-    h_refs, refs = refs[:near], refs[near:]
-    sum_ref, left_ref, right_ref, shift_ref, rows_ref, hs_ref, hd_ref, wr_ref, t_ref = refs
+    sg_refs, refs = refs[:plan.lead_steps], refs[plan.lead_steps:]
+    mates = len(flips[0]) - 1
+    mate_refs, refs = refs[:mates], refs[mates:]
+    sum_ref, left_ref, right_ref, shift_ref, rows_ref, hs_ref, hd_ref, wr_ref = refs[:8]
+    t_ref, h_ref, weight_ref, count_ref, sems = refs[8:]
     masks = Masks(orbitals)
+    own_copy = fetch(own_ref, h_ref, sems.at[0])
+    weight_copy = fetch(weights_ref, weight_ref, sems.at[1])
+    count_copy = fetch(counts_ref, count_ref, sems.at[2])
     freq_pos, group_pos, _ = plan.positions()
-    for place in range(plan.sub):
+    for place in range(plan.lead):
+        sg_ref = sg_refs[place // plan.sub]
+        member = place % plan.sub
         prepare_frequency(
-            plan, masks, place, sg_ref[0, place], sg_ref[1, place], place,
+            plan, masks, place, sg_ref[0, member], sg_ref[1, member], place,
             left_ref, right_ref, shift_ref, rows_ref,
         )
+
+    def load_piece(piece, source_ref):
+        for local in range(k_local):
+            place = piece * k_local + local
+            matrix = source_ref[local]
+            high, low = split_bf16(block_form(matrix, masks.sign))
+            hs_ref[place] = left_tile(high, low)
+            hd_ref[pl.ds(place, 1), :] = diagonal_row(masks, matrix)
+            t_ref[place] = product(left_ref[...], right_tile(high, low))
+
+    for piece, mate_ref in enumerate(mate_refs):
+        load_piece(piece + 1, mate_ref)
+    own_copy.wait()
+    load_piece(0, h_ref)
+    weight_copy.wait()
+    count_copy.wait()
     for group, members in enumerate(flips):
         for piece, (x_flip, c_flip) in enumerate(members):
             first_k = ((freq_pos ^ x_flip) * plan.group_devs + (group_pos ^ c_flip)) * k_local
             for local in range(k_local):
-                weight = weights_ref[first_k + local].astype(jnp.float32)
+                weight = weight_ref[first_k + local].astype(jnp.float32)
                 place = piece * k_local + local
                 wr_ref[group, pl.ds(place, 1), :] = jnp.full((1, plan.width), weight, jnp.float32)
-    for piece in range(near):
-        for local in range(k_local):
-            place = piece * k_local + local
-            matrix = h_refs[piece][local]
-            high, low = split_bf16(block_form(matrix, masks.sign))
-            hs_ref[place] = left_tile(high, low)
-            hd_ref[pl.ds(place, 1), :] = diagonal_row(masks, matrix)
-            t_ref[place] = product(left_ref[...], right_tile(high, low))
 
     def one_frequency(place, carry):
         offset = pl.multiple_of(place * orbitals, orbitals)
@@ -228,39 +251,41 @@
             lambda item: t_ref[item, pl.ds(offset, orbitals), :],
             hd_ref[...], wr_ref[0], jnp.zeros((orbitals, plan.width), jnp.float32),
         )
-        run_counts(counts_ref[plan.freq_of(place)], accumulate, store)
+        run_counts(count_ref[plan.freq_of(place)], accumulate, store)
         return carry
 
-    lax.fori_loop(0, plan.sub, one_frequency, 0)
+    lax.fori_loop(0, plan.lead, one_frequency, 0)
 
 
 def near_kernel(plan, counts_ref, *refs):
-    orbitals, width, sub = plan.orbitals, plan.width, plan.sub
-    steps = plan.z_devs - 1
+    orbitals, width, sub, lead = plan.orbitals, plan.width, plan.sub, plan.lead
+    steps = plan.z_devs - plan.lead_steps
     sg_refs, refs = refs[:steps], refs[steps:]
     old_refs, refs = refs[:5], refs[5:]
     hs_ref, hd_ref, wr_ref = refs[:3]
-    new_refs, (t_ref,) = refs[3:8], refs[8:]
+    new_refs, (t_ref, count_ref, sems) = refs[3:8], refs[8:]
     sum_ref, left_ref, right_ref, shift_ref, rows_ref = new_refs
     masks = Masks(orbitals)
-    left_ref[pl.ds(0, sub * orbitals), :] = old_refs[1][...]
-    for old_ref, new_ref in zip(old_refs, new_refs):
-        if old_ref is not old_refs[1]:
-            for place in range(sub):
-                new_ref[place] = old_ref[place]
-    for place in range(sub, plan.freqs):
-        sg_ref = sg_refs[place // sub - 1]
+    count_copy = fetch(counts_ref, count_ref, sems.at[0])
+    for place in range(lead, plan.freqs):
+        sg_ref = sg_refs[place // sub - plan.lead_steps]
         prepare_frequency(
             plan, masks, place, sg_ref[0, place % sub], sg_ref[1, place % sub], place,
             left_ref, right_ref, shift_ref, rows_ref,
         )
-    lefts = left_ref[pl.ds(sub * orbitals, (plan.freqs - sub) * orbitals), :]
+    lefts = left_ref[pl.ds(lead * orbitals, (plan.freqs - lead) * orbitals), :]
     for item in range(plan.k_total):
         tile = hs_ref[item]
         t_ref[item] = product(lefts, right_tile(tile[:, :width], tile[:, width:]))
+    left_ref[pl.ds(0, lead * orbitals), :] = old_refs[1][...]
+    for old_ref, new_ref in zip(old_refs, new_refs):
+        if old_ref is not old_refs[1]:
+            for place in range(lead):
+                new_ref[place] = old_ref[place]
+    count_copy.wait()
 
     def one_frequency(place, carry):
-        offset = pl.multiple_of((place - sub) * orbitals, orbitals)
+        offset = pl.multiple_of((place - lead) * orbitals, orbitals)
 
         def store(total):
             sum_ref[place] = total
@@ -270,10 +295,10 @@
             lambda item: t_ref[item, pl.ds(offset, orbitals), :],
             hd_ref[...], wr_ref[0], jnp.zeros((orbitals, width), jnp.float32),
         )
-        run_counts(counts_ref[plan.freq_of(place)], accumulate, store)
+        run_counts(count_ref[plan.freq_of(place)], accumulate, store)
         return carry
 
-    lax.fori_loop(sub, plan.freqs, one_frequency, 0)
+    lax.fori_loop(lead, plan.freqs, one_frequency, 0)
 
 
 def far_kernel(plan, group, pieces, counts_ref, *refs):
@@ -281,8 +306,9 @@
     half = orbitals // 2
     h_refs, refs = refs[:pieces], refs[pieces:]
     old_ref, left_ref, right_ref, shift_ref, rows_ref, wr_ref = refs[:6]
-    out_ref, t_ref, hd_ref, r_ref, plane_ref = refs[6:]
+    out_ref, t_ref, hd_ref, r_ref, plane_ref, count_ref, sems = refs[6:]
     masks = Masks(orbitals)
+    count_copy = fetch(counts_ref, count_ref, sems.at[0])
     for piece in range(pieces):
         for local in range(k_local):
             place = piece * k_local + local
@@ -290,34 +316,40 @@
             hd_ref[pl.ds(place, 1), :] = diagonal_row(masks, matrix)
             tile = right_tile(*split_bf16(block_form(matrix, masks.sign)))
             t_ref[place] = product(left_ref[...], tile)
+    count_copy.wait()
 
     def one_frequency(place, carry):
         offset = pl.multiple_of(place * orbitals, orbitals)
 
         def store(total):
-            tile = right_ref[place]
-            right = right_tile(tile[:, :width], tile[:, width:])
-            r_ref[...] = product(left_tile(*split_bf16(total)), right)
-
-        if pieces:
-            accumulate = sum_points(
-                plan, masks, rows_ref[place], shift_ref[place],
-                lambda item: t_ref[item, pl.ds(offset, orbitals), :],
-                hd_ref[...], wr_ref[group], old_ref[place],
-            )
-            run_counts(counts_ref[plan.freq_of(place)], accumulate, store)
-        else:
-            store(old_ref[place])
-        even = r_ref[pl.ds(0, half, stride=2), :]
-        odd = r_ref[pl.ds(1, half, stride=2), :]
+            r_ref[place] = total
+
+        accumulate = sum_points(
+            plan, masks, rows_ref[place], shift_ref[place],
+            lambda item: t_ref[item, pl.ds(offset, orbitals), :],
+            hd_ref[...], wr_ref[group], old_ref[place],
+        )
+        run_counts(count_ref[plan.freq_of(place)], accumulate, store)
+        return carry
+
+    if pieces:
+        lax.fori_loop(0, freqs, one_frequency, 0)
+    totals = r_ref if pieces else old_ref
+    greens = []
+    for place in range(freqs):
+        tile = right_ref[place]
+        right = right_tile(tile[:, :width], tile[:, width:])
+        greens.append(product(left_tile(*split_bf16(totals[place])), right))
+    for place, green in enumerate(greens):
+        r_ref[place] = green
+    for place in range(freqs):
+        even = r_ref[place, pl.ds(0, half, stride=2), :]
+        odd = r_ref[place, pl.ds(1, half, stride=2), :]
         plane = plan.plane_of(place)
         real_rows = pl.multiple_of(plane * half, half)
         imag_rows = pl.multiple_of((freqs + plane) * half, half)
         plane_ref[pl.ds(real_rows, half), :] = jnp.where(masks.left_row, even, swap_halves(odd))
         plane_ref[pl.ds(imag_rows, half), :] = jnp.where(masks.left_row, swap_halves(even), odd)
-        return carry
-
-    lax.fori_loop(0, freqs, one_frequency, 0)
     for line in range(half):
         out_ref[line] = plane_ref[pl.ds(line, 2 * freqs, stride=half), :]
 
@@ -370,7 +402,8 @@
 
     own = jnp.stack([self_energy, guess_factor])
     own = lax.dynamic_slice_in_dim(own, c_pos * sub, sub, 1)
-    others = [z_move(own, step) for step in range(1, z_devs)]
+    others = [z_move(own, step) for step in reversed(range(plan.lead_steps, z_devs))][::-1]
+    leading = [own] + [z_move(own, step) for step in range(1, plan.lead_steps)]
     near, near_flips, far, far_flips = [hamiltonian], [(0, 0)], [], []
     if plan.c_devs == 2:
         near.append(core_flip(hamiltonian))
@@ -386,7 +419,13 @@
     k_rows = -(-plan.k_total // 8) * 8
 
     vmem = pl.BlockSpec(memory_space=pltpu.VMEM)
-    smem = pl.BlockSpec(memory_space=pltpu.SMEM)
+    outside = pl.BlockSpec(memory_space=pltpu.HBM)
+
+    def in_hbm(values):
+        return pltpu.with_memory_space_constraint(values, pltpu.HBM)
+
+    count_scratch = pltpu.SMEM(counts.shape, counts.dtype)
+    far_counts = in_hbm(counts)
     params = pltpu.CompilerParams(vmem_limit_bytes=40 * 1024 * 1024)
 
     estimate = pl.CostEstimate(flops=COST, bytes_accessed=1 << 20, transcendentals=0)
@@ -406,48 +445,62 @@
             f32(places, 8, width),
         ]
 
-    outputs = shared(sub) + [
+    outputs = shared(plan.lead) + [
         bf16(plan.k_total, 2 * orbitals, 2 * width), f32(k_rows, width), f32(2, k_rows, width)
     ]
     lead = pl.pallas_call(
         functools.partial(first_kernel, plan, flips),
         out_shape=outputs,
-        in_specs=[smem, smem] + [vmem] * (1 + len(near)),
+        in_specs=[outside] * 3 + [vmem] * (len(leading) + len(near) - 1),
         out_specs=[vmem] * len(outputs),
-        scratch_shapes=[pltpu.VMEM((plan.k_total, sub * orbitals, width), jnp.float32)],
+        scratch_shapes=[
+            pltpu.VMEM((plan.k_total, plan.lead * orbitals, width), jnp.float32),
+            pltpu.VMEM((k_local, orbitals, width), jnp.float32),
+            pltpu.SMEM(weights.shape, weights.dtype),
+            count_scratch,
+            pltpu.SemaphoreType.DMA((3,)),
+        ],
         compiler_params=params,
         cost_estimate=estimate,
         name="first",
     )
-    *old, h_tiles, h_diags, w_rows = lead(weights, counts, own, *near)
+    *old, h_tiles, h_diags, w_rows = lead(
+        in_hbm(weights), far_counts, in_hbm(hamiltonian), *leading, *near[1:]
+    )
     outputs = shared(freqs)
     shares = pl.pallas_call(
         functools.partial(near_kernel, plan),
         out_shape=outputs,
-        in_specs=[smem] + [vmem] * (len(others) + len(old) + 3),
+        in_specs=[outside] + [vmem] * (len(others) + len(old) + 3),
         out_specs=[vmem] * len(outputs),
-        scratch_shapes=[pltpu.VMEM((plan.k_total, (freqs - sub) * orbitals, width), jnp.float32)],
+        scratch_shapes=[
+            pltpu.VMEM((plan.k_total, (freqs - plan.lead) * orbitals, width), jnp.float32),
+            count_scratch,
+            pltpu.SemaphoreType.DMA((1,)),
+        ],
         compiler_params=params,
         cost_estimate=estimate,
         name="near",
-    )(counts, *others, *old, h_tiles, h_diags, w_rows)
+    )(far_counts, *others, *old, h_tiles, h_diags, w_rows)
     if far and plan.c_devs == 2:
         crossed, _ = lax.optimization_barrier((far[0], w_rows))
         far.append(core_flip(crossed))
     partial_sums = pl.pallas_call(
         functools.partial(far_kernel, plan, 1, len(far)),
         out_shape=f32(half, 2 * freqs, width),
-        in_specs=[smem] + [vmem] * (len(far) + len(shares) + 1),
+        in_specs=[outside] + [vmem] * (len(far) + len(shares) + 1),
         out_specs=vmem,
         scratch_shapes=[
             pltpu.VMEM((plan.k_total, freqs * orbitals, width), jnp.float32),
             pltpu.VMEM((k_rows, width), jnp.float32),
-            pltpu.VMEM((orbitals, width), jnp.float32),
+            pltpu.VMEM((freqs, orbitals, width), jnp.float32),
             pltpu.VMEM((2 * freqs * half, width), jnp.float32),
+            count_scratch,
+            pltpu.SemaphoreType.DMA((1,)),
         ],
         compiler_params=params,
         name="far",
-    )(counts, *far, *shares, w_rows)
+    )(far_counts, *far, *shares, w_rows)
 
     share = width // pair_block
     outgoing = partial_sums.reshape(half, 2 * freqs, share, pair_block).transpose(0, 2, 1, 3)

time: 45.1 us -> 43.8 us (0.971)
  waiting for transfers between devices: 9.54 us -> 7.18 us
  starting transfers between devices: 7.39 us -> 8.63 us
  blocking collectives: 13.1 us -> 14.3 us
  local copies, waits for them, and re-layouts: 0.97 us -> 0 us
    ppermute x1, waiting for transfers between devices: 3.47 us -> 0.01 us  [x_flip(): lax.ppermute(values, 'freq', [(i, i ^ 1) for i in range(plan.freq_devs)])]
    all_to_all x1, blocking collectives: 13.1 us -> 14.3 us  [local_green(): arrived = lax.all_to_all(outgoing, ('freq', 'kgrp'), 0, 0, tiled=True)]
    ppermute x3, starting transfers between devices: 4.42 us -> 5.58 us  [z_move(): return lax.ppermute(values, 'freq', pairs)]
    ppermute x3, waiting for transfers between devices: 6.06 us -> 7.17 us  [z_move(): return lax.ppermute(values, 'freq', pairs)]
    unnamed x6 -> x0, local copies, waits for them, and re-layouts: 0.97 us -> none
    pallas_call x1, Pallas kernels: 2.72 us -> 3.57 us  [local_green(): lead(in_hbm(weights), far_counts, in_hbm(hamiltonian), *leading, *near[1:])]
    pallas_call x1, Pallas kernels: 3.03 us -> 2.3 us  [local_green(): pl.pallas_call(functools.partial(near_kernel, plan), out_shape=outputs, i...]
    pallas_call x1, Pallas kernels: 5.57 us -> 5.07 us  [local_green(): pl.pallas_call(functools.partial(far_kernel, plan, 1, len(far)), out_shap...]
  transfers between devices with their start and end apart: 6 -> 6, of which waited for: 4 -> 2; matrix products, arithmetic and copies ran while one was open for 2% -> 2% of each run, Pallas kernels for 13% -> 13%
where the time goes in v4:
time: 43.8 us; the launch traced here: 43.5 us
  blocking collectives  14.3 us (33%)
  Pallas kernels  12.6 us (29%)
  starting transfers between devices  8.63 us (20%)
  waiting for transfers between devices  7.18 us (16%)
  other arithmetic  0.78 us (2%)
    all_to_all x1, blocking collectives, local_green(): arrived = lax.all_to_all(outgoing, ('freq', 'kgrp'), 0, 0, tiled=True)  14.3 us
    ppermute x3, waiting for transfers between devices, z_move(): return lax.ppermute(values, 'freq', pairs)  7.17 us
    ppermute x3, starting transfers between devices, z_move(): return lax.ppermute(values, 'freq', pairs)  5.58 us
    pallas_call x1, Pallas kernels, local_green(): pl.pallas_call(functools.partial(far_kernel, plan, 1, len(far)), out_shap...  5.07 us
    pallas_call x1, Pallas kernels, local_green(): lead(in_hbm(weights), far_counts, in_hbm(hamiltonian), *leading, *near[1:])  3.57 us
    ppermute x1, starting transfers between devices, x_flip(): lax.ppermute(values, 'freq', [(i, i ^ 1) for i in range(plan.freq_devs)])  2.48 us
    pallas_call x1, Pallas kernels, local_green(): pl.pallas_call(functools.partial(near_kernel, plan), out_shape=outputs, i...  2.3 us
    pallas_call x1, Pallas kernels, local_green(): pl.pallas_call(functools.partial(final_kernel, (z_devs, x_devs, plan.y_de...  1.65 us
  transfers between devices with their start and end apart: 6, of which 2 were waited for; matrix products, arithmetic and copies ran while one was open for 2% of the time, Pallas kernels for 13%

profile of v4, /device:TPU:0, one launch (start us, length us, event | category | flops | bytes accessed | tf_op | source)
XLA Modules:
  0.0 43.5 jit_solution(4610926040769413169)
XLA Ops:
  0.0 0.5 %collective-permute-start.2 = (f32[8,64,128]{2,1,0:T(8,128)}, f32[8,64,128]{2,1,0:T(8,128)S(1)}, u32[]{:S(2)}, u32[]{:S(2)}) collective-permute-start(f32[8,64,128]{2,1,0:T(8,128)} %own_ref.1), channel_id=1, source_target_pairs={{0,1},{1,0},{2,3},{3,2},{4,5},{5,4},{6,7},{7,6},{8,9},{9,8},{10,11... | collective-permute-start | bytes 786440 | tf_op jit(solution)/shard_map/ppermute | solution.py:390
  0.5 0.8 %fusion.refs_0_ = f32[2,1,64,128]{3,2,1,0:T(8,128)S(1)} fusion(s32[]{:T(128)S(6)} %select_n.11, f32[1,2,64,128]{3,2,1,0:T(8,128)} %bitcast.4, f32[1,2,64,128]{3,2,1,0:T(8,128)} %bitcast.5), kind=kLoop, calls=%fused_computation.2 | loop fusion | flops 16384 | bytes 196612 | tf_op jit(solution)/shard_map/stack | solution.py:403
  1.3 2.5 %collective-permute-start = (f32[8,64,128]{2,1,0:T(8,128)}, f32[8,64,128]{2,1,0:T(8,128)S(1)}, u32[]{:S(2)}, u32[]{:S(2)}) collective-permute-start(f32[8,64,128]{2,1,0:T(8,128)} %own_ref.1), channel_id=1, source_target_pairs={{0,4},{4,0},{8,12},{12,8},{16,20},{20,16},{24,28},{28,24},{1,5},{5... | collective-permute-start | bytes 786440 | tf_op jit(solution)/shard_map/ppermute | solution.py:393
  3.8 1.6 %collective-permute-start.1 = (f32[2,1,64,128]{3,2,1,0:T(8,128)S(1)}, f32[2,1,64,128]{3,2,1,0:T(8,128)S(1)}, u32[]{:S(2)}, u32[]{:S(2)}) collective-permute-start(f32[2,1,64,128]{3,2,1,0:T(8,128)S(1)} %fusion.refs_0_), channel_id=1, source_target_pairs={{0,8},{4,12},{8,0},{12,4},{16,24},{20,28},{24,16},{28,20},{1,9},{5... | collective-permute-start | bytes 196616 | tf_op jit(solution)/shard_map/ppermute | solution.py:401
  5.3 2.7 %collective-permute-done.1.refs_1_ = f32[2,1,64,128]{3,2,1,0:T(8,128)S(1)} collective-permute-done((f32[2,1,64,128]{3,2,1,0:T(8,128)S(1)}, f32[2,1,64,128]{3,2,1,0:T(8,128)S(1)}, u32[]{:S(2)}, u32[]{:S(2)}) %collective-permute-start.1) | collective-permute-done | bytes 65568 | tf_op jit(solution)/shard_map/ppermute | solution.py:401
  8.0 0.0 collective-permute-done.2.refs_2_
  8.0 3.6 %first.1 = (f32[2,64,128]{2,1,0:T(8,128)S(1)}, bf16[128,256]{1,0:T(8,128)(2,1)S(1)}, bf16[2,128,256]{2,1,0:T(8,128)(2,1)S(1)}, f32[2,64,128]{2,1,0:T(8,128)S(1)}...) custom-call(s32[256]{0:T(256)} %weights_ref.1, ...), custom_call_target="tpu_custom_call" | custom-call | flops 400000000 | bytes 1048576 | tf_op jit(solution)/shard_map/first/pallas_call | solution.py:467
  11.6 0.0 collective-permute-done.refs_0_
  11.6 0.1 collective-permute-start.3
  11.7 2.1 %collective-permute-start.4 = (f32[2,1,64,128]{3,2,1,0:T(8,128)S(1)}, f32[2,1,64,128]{3,2,1,0:T(8,128)S(1)}, u32[]{:S(2)}, u32[]{:S(2)}) collective-permute-start(f32[2,1,64,128]{3,2,1,0:T(8,128)S(1)} %fusion.refs_0_), channel_id=1, source_target_pairs={{0,16},{4,20},{8,24},{12,28},{16,0},{20,4},{24,8},{28,12},{1,17},{... | collective-permute-start | bytes 196616 | tf_op jit(solution)/shard_map/ppermute | solution.py:401
  13.8 1.9 %collective-permute-start.5 = (f32[2,1,64,128]{3,2,1,0:T(8,128)S(1)}, f32[2,1,64,128]{3,2,1,0:T(8,128)S(1)}, u32[]{:S(2)}, u32[]{:S(2)}) collective-permute-start(f32[2,1,64,128]{3,2,1,0:T(8,128)S(1)} %fusion.refs_0_), channel_id=1, source_target_pairs={{0,24},{4,28},{8,16},{12,20},{16,8},{20,12},{24,0},{28,4},{1,25},{... | collective-permute-start | bytes 196616 | tf_op jit(solution)/shard_map/ppermute | solution.py:401
  15.7 4.5 %collective-permute-done.4.refs_0_ = f32[2,1,64,128]{3,2,1,0:T(8,128)S(1)} collective-permute-done((f32[2,1,64,128]{3,2,1,0:T(8,128)S(1)}, f32[2,1,64,128]{3,2,1,0:T(8,128)S(1)}, u32[]{:S(2)}, u32[]{:S(2)}) %collective-permute-start.4) | collective-permute-done | bytes 65568 | tf_op jit(solution)/shard_map/ppermute | solution.py:401
  20.2 0.0 collective-permute-done.5.refs_1_
  20.2 2.3 %near.1 = (f32[4,64,128]{2,1,0:T(8,128)S(1)}, bf16[256,256]{1,0:T(8,128)(2,1)S(1)}, bf16[4,128,256]{2,1,0:T(8,128)(2,1)S(1)}, f32[4,64,128]{2,1,0:T(8,128)S(1)}, f32[4,8,128]{2,1,0:T(8,128)S(1)}) custom-call(s32[16]{0:T(128)} %counts_ref.5, f32[2,1,64,128]{3,2,1,0:T(8,128)S(1)} %collective-permute-done.4.refs_0_, ...), custom_call_target="tpu_custom_call" | custom-call | flops 400000000 | bytes 1048576 | tf_op jit(solution)/shard_map/near/pallas_call | solution.py:471
  22.5 0.0 collective-permute-done.3.refs_1_
  22.5 5.1 %far.1 = f32[32,8,128]{2,1,0:T(8,128)S(1)} custom-call(s32[16]{0:T(128)} %counts_ref.5, f32[8,64,128]{2,1,0:T(8,128)S(1)} %collective-permute-done.refs_0_, f32[8,64,128]{2,1,0:T(8,128)S(1)} %collective-permute-done.3.refs_1_, f32[4,64,128]{2,1,0:T(8,128)S(1)} %get-tuple-element.30.refs_2_, bf16[256,256]{1,0:T(8,128)(2,1)S(1)} %get-tuple-element.31.refs_3_, ...), custom_call_target="tpu_custom_call" | custom-call | tf_op jit(solution)/shard_map/far/pallas_call | solution.py:488
  27.6 14.3 %all_to_all.5.parts_ref = f32[32,8,128]{2,1,0:T(8,128)} all-to-all(f32[32,8,128]{2,1,0:T(8,128)S(1)} %far.1), channel_id=1, replica_groups=mesh['freq'=8,'kgrp'=4] {'freq','kgrp'}, dimensions={0} | all-to-all | bytes 262144 | tf_op jit(solution)/shard_map/all_to_all | solution.py:508
  41.9 1.7 %collect.1 = f32[32,128]{1,0:T(8,128)} custom-call(s32[1,256]{1,0:T(1,128)} %bitcast.6, f32[32,8,128]{2,1,0:T(8,128)} %all_to_all.5.parts_ref), custom_call_target="tpu_custom_call" | custom-call | tf_op jit(solution)/shard_map/collect/pallas_call | solution.py:509
Async XLA Ops:
  0.0 8.0 %collective-permute-start.2 = (f32[8,64,128]{2,1,0:T(8,128)}, f32[8,64,128]{2,1,0:T(8,128)S(1)}, u32[]{:S(2)}, u32[]{:S(2)}) collective-permute-start(f32[8,64,128]{2,1,0:T(8,128)} %own_ref.1), channel_id=1, source_target_pairs={{0,1},{1,0},{2,3},{3,2},{4,5},{5,4},{6,7},{7,6},{8,9},{9,8},{10,11... | collective-permute-start | bytes 786440 | tf_op jit(solution)/shard_map/ppermute | solution.py:390
  1.3 10.3 %collective-permute-start = (f32[8,64,128]{2,1,0:T(8,128)}, f32[8,64,128]{2,1,0:T(8,128)S(1)}, u32[]{:S(2)}, u32[]{:S(2)}) collective-permute-start(f32[8,64,128]{2,1,0:T(8,128)} %own_ref.1), channel_id=1, source_target_pairs={{0,4},{4,0},{8,12},{12,8},{16,20},{20,16},{24,28},{28,24},{1,5},{5... | collective-permute-start | bytes 786440 | tf_op jit(solution)/shard_map/ppermute | solution.py:393
  3.8 4.3 %collective-permute-start.1 = (f32[2,1,64,128]{3,2,1,0:T(8,128)S(1)}, f32[2,1,64,128]{3,2,1,0:T(8,128)S(1)}, u32[]{:S(2)}, u32[]{:S(2)}) collective-permute-start(f32[2,1,64,128]{3,2,1,0:T(8,128)S(1)} %fusion.refs_0_), channel_id=1, source_target_pairs={{0,8},{4,12},{8,0},{12,4},{16,24},{20,28},{24,16},{28,20},{1,9},{5... | collective-permute-start | bytes 196616 | tf_op jit(solution)/shard_map/ppermute | solution.py:401
  11.6 10.9 %collective-permute-start.3 = (f32[8,64,128]{2,1,0:T(8,128)S(1)}, f32[8,64,128]{2,1,0:T(8,128)S(1)}, u32[]{:S(2)}, u32[]{:S(2)}) collective-permute-start(f32[8,64,128]{2,1,0:T(8,128)S(1)} %collective-permute-done.refs_0_), channel_id=1, source_target_pairs={{0,1},{1,0},{2,3},{3,2},{4,5},{5,4},{6,7},{7,6},{8,9},{9,8},{10,11... | collective-permute-start | bytes 786440 | tf_op jit(solution)/shard_map/ppermute | solution.py:390
  11.7 8.5 %collective-permute-start.4 = (f32[2,1,64,128]{3,2,1,0:T(8,128)S(1)}, f32[2,1,64,128]{3,2,1,0:T(8,128)S(1)}, u32[]{:S(2)}, u32[]{:S(2)}) collective-permute-start(f32[2,1,64,128]{3,2,1,0:T(8,128)S(1)} %fusion.refs_0_), channel_id=1, source_target_pairs={{0,16},{4,20},{8,24},{12,28},{16,0},{20,4},{24,8},{28,12},{1,17},{... | collective-permute-start | bytes 196616 | tf_op jit(solution)/shard_map/ppermute | solution.py:401
  13.8 6.4 %collective-permute-start.5 = (f32[2,1,64,128]{3,2,1,0:T(8,128)S(1)}, f32[2,1,64,128]{3,2,1,0:T(8,128)S(1)}, u32[]{:S(2)}, u32[]{:S(2)}) collective-permute-start(f32[2,1,64,128]{3,2,1,0:T(8,128)S(1)} %fusion.refs_0_), channel_id=1, source_target_pairs={{0,24},{4,28},{8,16},{12,20},{16,8},{20,12},{24,0},{28,4},{1,25},{... | collective-permute-start | bytes 196616 | tf_op jit(solution)/shard_map/ppermute | solution.py:401
